TPU v7x, 16 devices: a whole 2x2x2 slice. The times are simulated.
16 devices in a mesh: tp: 16 (over z, y, x, core).
Axes of the slice: x: 2, y: 2, z: 2, core: 2. Of those that a mesh axis runs over, the one named last changes fastest.
Arguments:
- tokens: int32 [2, 128], replicated
- lengths: int32 [128], replicated
- embedding: bfloat16 [51200, 2560], P('tp')
- ln_scale: float32 [2, 2560], replicated
- w_q: bfloat16 [2, 2560, 32, 80], P(None, None, 'tp')
- w_kv: bfloat16 [2, 2560, 160], replicated
- w_o: bfloat16 [2, 32, 80, 2560], P(None, 'tp')
- w_gate: bfloat16 [2, 2560, 10240], P(None, None, 'tp')
- w_up: bfloat16 [2, 2560, 10240], P(None, None, 'tp')
- w_down: bfloat16 [2, 10240, 2560], P(None, 'tp')
- final_scale: float32 [2560], replicated
- k_cache: bfloat16 [2, 128, 2048, 80], P(None, 'tp')
- v_cache: bfloat16 [2, 128, 2048, 80], P(None, 'tp')
Outputs:
- output 1: float32 [2, 128, 51200], P(None, None, 'tp')
- output 2: bfloat16 [2, 128, 2048, 80], P(None, 'tp')
- output 3: bfloat16 [2, 128, 2048, 80], P(None, 'tp')
All inputs are finite; a program needn't handle non-finite values.
Results may differ from a plain program's by a relative error of at most 0.00684216.
Values are sent between devices in bfloat16 or wider.
A program may use at most 1 GiB of HBM per device.

v0:
```python
import jax
import jax.numpy as jnp
from jax import lax
from jax.sharding import PartitionSpec as P

LN_EPS = 1e-6


def layer_norm(residual, ln_gain):
    x_f32 = residual.astype(jnp.float32)
    row_mean = jnp.mean(x_f32, axis=-1, keepdims=True)
    centred = x_f32 - row_mean
    row_var = jnp.mean(centred * centred, axis=-1, keepdims=True)
    return (centred * lax.rsqrt(row_var + LN_EPS) * ln_gain).astype(jnp.bfloat16)


def rotary(features, positions):
    half_dim = features.shape[-1] // 2
    inv_freq = 10000.0 ** (-jnp.arange(half_dim, dtype=jnp.float32) / half_dim)
    angles = positions[..., None].astype(jnp.float32) * inv_freq
    cos_t = jnp.cos(angles)
    sin_t = jnp.sin(angles)
    lo_half = features[..., :half_dim]
    hi_half = features[..., half_dim:]
    return jnp.concatenate([lo_half * cos_t - hi_half * sin_t, lo_half * sin_t + hi_half * cos_t], axis=-1)


def write_rows(cache, new_rows, positions):
    return jax.vmap(lambda seq_cache, new_row, at_pos: lax.dynamic_update_slice(seq_cache, new_row[None], (at_pos, 0)))(cache, new_rows, positions)


def solution(mesh):
    def device_fn(tokens, lengths, embedding, ln_scale, w_q, w_kv, w_o, w_gate, w_up, w_down, final_scale, k_cache, v_cache):
        my_rank = lax.axis_index('tp')
        num_steps = tokens.shape[0]
        vocab_local = embedding.shape[0]
        model_dim = embedding.shape[1]
        layers, batch_local, seq_len, head_dim = k_cache.shape
        row_start = my_rank * batch_local
        local_len = lax.dynamic_slice_in_dim(lengths, row_start, batch_local)
        key_pos = lax.broadcasted_iota(jnp.int32, (1, 1, seq_len), 2)
        k_layers = [k_cache[layer_idx] for layer_idx in range(layers)]
        v_layers = [v_cache[layer_idx] for layer_idx in range(layers)]
        step_logits = []
        for step_idx in range(num_steps):
            positions = lengths + step_idx
            local_pos = local_len + step_idx
            tok_local = tokens[step_idx] - my_rank * vocab_local
            in_shard = (tok_local >= 0) & (tok_local < vocab_local)
            emb_rows = jnp.take(embedding, jnp.clip(tok_local, 0, vocab_local - 1), axis=0)
            emb_rows = jnp.where(in_shard[:, None], emb_rows, jnp.zeros_like(emb_rows))
            residual = lax.psum_scatter(emb_rows, 'tp', scatter_dimension=1, tiled=True)
            for layer_idx in range(layers):
                full_resid = lax.all_gather(residual, 'tp', axis=1, tiled=True)
                normed = layer_norm(full_resid, ln_scale[layer_idx])
                q_raw = jnp.einsum('bd,dhc->bhc', normed, w_q[layer_idx], preferred_element_type=jnp.float32)
                queries = rotary(q_raw, positions[:, None]).astype(jnp.bfloat16)
                normed_local = lax.dynamic_slice_in_dim(normed, row_start, batch_local, axis=0)
                kv_new = jnp.dot(normed_local, w_kv[layer_idx], preferred_element_type=jnp.float32)
                k_new = rotary(kv_new[:, :head_dim], local_pos).astype(jnp.bfloat16)
                v_new = kv_new[:, head_dim:].astype(jnp.bfloat16)
                k_layers[layer_idx] = write_rows(k_layers[layer_idx], k_new, local_pos)
                v_layers[layer_idx] = write_rows(v_layers[layer_idx], v_new, local_pos)
                seq_queries = lax.all_to_all(queries, 'tp', 0, 1, tiled=True)
                scores = jnp.einsum('bhc,bsc->bhs', seq_queries, k_layers[layer_idx], preferred_element_type=jnp.float32) * head_dim ** -0.5
                scores = jnp.where(key_pos <= local_pos[:, None, None], scores, -jnp.inf)
                attn_probs = jax.nn.softmax(scores, axis=-1).astype(jnp.bfloat16)
                seq_out = jnp.einsum('bhs,bsc->bhc', attn_probs, v_layers[layer_idx], preferred_element_type=jnp.float32).astype(jnp.bfloat16)
                head_out = lax.all_to_all(seq_out, 'tp', 1, 0, tiled=True)
                attn_part = jnp.einsum('bhc,hcd->bd', head_out, w_o[layer_idx], preferred_element_type=jnp.float32)
                gate_proj = jnp.dot(normed, w_gate[layer_idx], preferred_element_type=jnp.float32)
                up_proj = jnp.dot(normed, w_up[layer_idx], preferred_element_type=jnp.float32)
                hidden = (jax.nn.silu(gate_proj) * up_proj).astype(jnp.bfloat16)
                mlp_part = jnp.dot(hidden, w_down[layer_idx], preferred_element_type=jnp.float32)
                block_sum = lax.psum_scatter(attn_part + mlp_part, 'tp', scatter_dimension=1, tiled=True)
                residual = (residual.astype(jnp.float32) + block_sum).astype(jnp.bfloat16)
            full_resid = lax.all_gather(residual, 'tp', axis=1, tiled=True)
            normed = layer_norm(full_resid, final_scale)
            logits = lax.dot_general(normed, embedding, (((1,), (1,)), ((), ())), preferred_element_type=jnp.float32)
            step_logits.append(logits * model_dim ** -0.5)
        return jnp.stack(step_logits), jnp.stack(k_layers), jnp.stack(v_layers)

    cache_spec = P(None, 'tp', None, None)
    in_specs = (P(), P(), P('tp', None), P(), P(None, None, 'tp', None), P(), P(None, 'tp', None, None), P(None, None, 'tp'), P(None, None, 'tp'), P(None, 'tp', None), P(), cache_spec, cache_spec)
    out_specs = (P(None, None, 'tp'), cache_spec, cache_spec)
    return jax.shard_map(device_fn, mesh=mesh, in_specs=in_specs, out_specs=out_specs, check_vma=False)
```

profile of v0, /device:TPU:0, one launch (start us, length us, event | category | flops | bytes accessed | tf_op | source)
XLA Modules:
  0.0 987.8 jit_solution(1811694875274203766)
XLA Ops:
  8.8 9.4 gather_fusion.1
  19.5 9.4 gather_fusion
  31.8 5.3 fusion.255
  37.1 3.1 fusion.256
  40.3 5.9 copy.178
  46.2 5.9 copy.179
  52.4 24.7 %reduce-scatter.13.cloned.1.call-done = bf16[128,160]{0,1:T(8,128)(2,1)} async-done(((bf16[128,2560]{0,1:T(8,128)(2,1)}), bf16[128,160]{0,1:T(8,128)(2,1)}) %reduce-scatter.13.cloned.1.call-update) | async-done | bytes 40976 | tf_op jit(solution)/shard_map/reduce_scatter | solution.py:52
  77.1 12.9 %all_gather.21 = bf16[128,2560]{0,1:T(8,128)(2,1)S(1)} all-gather(bf16[128,160]{0,1:T(8,128)(2,1)} %reduce-scatter.13.cloned.1.call-done), channel_id=1, replica_groups=mesh['tp'=16] {'tp'}, dimensions={1}, use_global_device_ids=true | all-gather | bytes 696320 | tf_op jit(solution)/shard_map/all_gather | solution.py:54
  90.7 41.8 %reduce-scatter.7.cloned.1.call-done = bf16[128,160]{0,1:T(8,128)(2,1)} async-done(((bf16[128,2560]{0,1:T(8,128)(2,1)}), bf16[128,160]{0,1:T(8,128)(2,1)}) %reduce-scatter.7.cloned.1.call-update) | async-done | bytes 40976 | tf_op jit(solution)/shard_map/reduce_scatter | solution.py:52
  132.5 13.1 %all_gather.18 = bf16[128,2560]{0,1:T(8,128)(2,1)S(1)} all-gather(bf16[128,160]{0,1:T(8,128)(2,1)} %reduce-scatter.7.cloned.1.call-done), channel_id=1, replica_groups=mesh['tp'=16] {'tp'}, dimensions={1}, use_global_device_ids=true | all-gather | bytes 696320 | tf_op jit(solution)/shard_map/all_gather | solution.py:54
  149.3 3.4 fusion.32
  156.6 65.0 %while.8 = (s32[]{:T(128)}, bf16[8,2048,80]{2,1,0:T(8,128)(2,1)}, s32[8,3]{0,1:T(4,128)S(1)}, bf16[8,1,80]{2,0,1:T(8,128)(2,1)S(1)}, s32[]{:T(128)}, /*index=5*/s32[3]{0:T(128)S(1)}, s32[]{:T(128)}) while((s32[]{:T(128)}, bf16[8,2048,80]{2,1,0:T(8,128)(2,1)}, s32[8,3]{0,1:T(4,128)S(1)}, bf16[8,1,80]{2,0,1:T(8,128)(2,1)S(1)}, s32[]{:T(128)}, ...), condition=%wide.while_cond, body=%wide.while_body.sunk | while | flops 99 | bytes 979 | solution.py:29
  221.6 4.5 copy.233
  226.1 64.0 %while.12 = (s32[]{:T(128)}, bf16[8,2048,80]{2,1,0:T(8,128)(2,1)}, s32[8,3]{0,1:T(4,128)S(1)}, bf16[8,1,80]{2,0,1:T(8,128)(2,1)S(1)}, s32[]{:T(128)}, /*index=5*/s32[3]{0:T(128)S(1)}, s32[]{:T(128)}) while((s32[]{:T(128)}, bf16[8,2048,80]{2,1,0:T(8,128)(2,1)}, s32[8,3]{0,1:T(4,128)S(1)}, bf16[8,1,80]{2,0,1:T(8,128)(2,1)S(1)}, s32[]{:T(128)}, ...), condition=%wide.while_cond.4, body=%wide.while_body.4.sunk | while | flops 99 | bytes 979 | solution.py:29
  290.1 64.5 %while.9 = (s32[]{:T(128)}, bf16[8,2048,80]{2,1,0:T(8,128)(2,1)}, s32[8,3]{0,1:T(4,128)S(1)}, bf16[8,1,80]{2,0,1:T(8,128)(2,1)S(1)}, s32[]{:T(128)}, /*index=5*/s32[3]{0:T(128)S(1)}, s32[]{:T(128)}) while((s32[]{:T(128)}, bf16[8,2048,80]{2,1,0:T(8,128)(2,1)}, s32[8,3]{0,1:T(4,128)S(1)}, bf16[8,1,80]{2,0,1:T(8,128)(2,1)S(1)}, s32[]{:T(128)}, ...), condition=%wide.while_cond.1, body=%wide.while_body.1.sunk | while | flops 99 | bytes 979 | solution.py:29
  354.8 3.7 fusion.57
  360.3 4.4 convolution_convert_fusion.3
  365.3 3.8 all-to-all-start.1
  370.0 4.8 all-to-all-done.1
  377.5 2.9 convolution_bitcast_fusion.3
  380.4 6.2 convolution_add_fusion.3
  386.5 68.1 %while.13 = (s32[]{:T(128)}, bf16[8,2048,80]{2,1,0:T(8,128)(2,1)}, s32[8,3]{0,1:T(4,128)S(1)}, bf16[8,1,80]{2,0,1:T(8,128)(2,1)S(1)}, s32[]{:T(128)}, /*index=5*/s32[3]{0:T(128)S(1)}, s32[]{:T(128)}) while((s32[]{:T(128)}, bf16[8,2048,80]{2,1,0:T(8,128)(2,1)}, s32[8,3]{0,1:T(4,128)S(1)}, bf16[8,1,80]{2,0,1:T(8,128)(2,1)S(1)}, s32[]{:T(128)}, ...), condition=%wide.while_cond.5, body=%wide.while_body.5.sunk | while | flops 99 | bytes 979 | solution.py:29
  454.7 3.7 fusion.55
  460.2 4.4 convolution_convert_fusion.1
  465.3 3.7 all-to-all-start.5
  469.1 3.4 fusion.30
  474.7 2.9 convolution_bitcast_fusion.1
  477.5 6.2 convolution_add_fusion.1
  483.7 4.1 copy.180
  487.8 5.9 copy.181
  494.7 13.8 %all_gather.19 = bf16[128,2560]{0,1:T(8,128)(2,1)S(1)} all-gather(bf16[128,160]{0,1:T(8,128)(2,1)S(1)} %add_convert_fusion.3), channel_id=1, replica_groups=mesh['tp'=16] {'tp'}, dimensions={1}, use_global_device_ids=true | all-gather | bytes 696320 | tf_op jit(solution)/shard_map/all_gather | solution.py:54
  509.2 30.0 %reduce-scatter.15.cloned.1.call-done = f32[128,160]{0,1:T(8,128)} async-done(((f32[128,2560]{0,1:T(8,128)}), f32[128,160]{0,1:T(8,128)}) %reduce-scatter.15.cloned.1.call-update) | async-done | bytes 81936 | tf_op jit(solution)/shard_map/reduce_scatter | solution.py:75
  540.1 13.2 %all_gather.22 = bf16[128,2560]{0,1:T(8,128)(2,1)S(1)} all-gather(bf16[128,160]{0,1:T(8,128)(2,1)S(1)} %add_convert_fusion.1), channel_id=1, replica_groups=mesh['tp'=16] {'tp'}, dimensions={1}, use_global_device_ids=true | all-gather | bytes 696320 | tf_op jit(solution)/shard_map/all_gather | solution.py:54
  557.0 3.4 fusion.22
  560.7 66.6 %while.10 = (s32[]{:T(128)}, bf16[8,2048,80]{2,1,0:T(8,128)(2,1)}, s32[8,3]{0,1:T(4,128)S(1)}, bf16[8,1,80]{2,0,1:T(8,128)(2,1)S(1)}, s32[]{:T(128)}, /*index=5*/s32[3]{0:T(128)S(1)}, s32[]{:T(128)}) while((s32[]{:T(128)}, bf16[8,2048,80]{2,1,0:T(8,128)(2,1)}, s32[8,3]{0,1:T(4,128)S(1)}, bf16[8,1,80]{2,0,1:T(8,128)(2,1)S(1)}, s32[]{:T(128)}, ...), condition=%wide.while_cond.2, body=%wide.while_body.2.sunk | while | flops 99 | bytes 979 | solution.py:29
  630.9 4.5 copy.257
  635.4 63.6 %while.14 = (s32[]{:T(128)}, bf16[8,2048,80]{2,1,0:T(8,128)(2,1)}, s32[8,3]{0,1:T(4,128)S(1)}, bf16[8,1,80]{2,0,1:T(8,128)(2,1)S(1)}, s32[]{:T(128)}, /*index=5*/s32[3]{0:T(128)S(1)}, s32[]{:T(128)}) while((s32[]{:T(128)}, bf16[8,2048,80]{2,1,0:T(8,128)(2,1)}, s32[8,3]{0,1:T(4,128)S(1)}, bf16[8,1,80]{2,0,1:T(8,128)(2,1)S(1)}, s32[]{:T(128)}, ...), condition=%wide.while_cond.6, body=%wide.while_body.6.sunk | while | flops 99 | bytes 979 | solution.py:29
  699.0 63.8 %while.11 = (s32[]{:T(128)}, bf16[8,2048,80]{2,1,0:T(8,128)(2,1)}, s32[8,3]{0,1:T(4,128)S(1)}, bf16[8,1,80]{2,0,1:T(8,128)(2,1)S(1)}, s32[]{:T(128)}, /*index=5*/s32[3]{0:T(128)S(1)}, s32[]{:T(128)}) while((s32[]{:T(128)}, bf16[8,2048,80]{2,1,0:T(8,128)(2,1)}, s32[8,3]{0,1:T(4,128)S(1)}, bf16[8,1,80]{2,0,1:T(8,128)(2,1)S(1)}, s32[]{:T(128)}, ...), condition=%wide.while_cond.3, body=%wide.while_body.3.sunk | while | flops 99 | bytes 979 | solution.py:29
  763.0 3.7 fusion.56
  767.2 3.8 convolution_convert_fusion.2
  772.4 3.7 all-to-all-start.3
  777.0 4.8 all-to-all-done.3
  786.1 5.8 convolution_add_fusion.2
  791.9 67.6 %while.15 = (s32[]{:T(128)}, bf16[8,2048,80]{2,1,0:T(8,128)(2,1)}, s32[8,3]{0,1:T(4,128)S(1)}, bf16[8,1,80]{2,0,1:T(8,128)(2,1)S(1)}, s32[]{:T(128)}, /*index=5*/s32[3]{0:T(128)S(1)}, s32[]{:T(128)}) while((s32[]{:T(128)}, bf16[8,2048,80]{2,1,0:T(8,128)(2,1)}, s32[8,3]{0,1:T(4,128)S(1)}, bf16[8,1,80]{2,0,1:T(8,128)(2,1)S(1)}, s32[]{:T(128)}, ...), condition=%wide.while_cond.7, body=%wide.while_body.7.sunk | while | flops 99 | bytes 979 | solution.py:29
  792.6 2.7 and_reduce_fusion.23
  817.9 2.7 and_reduce_fusion.23
  859.6 3.7 fusion.54
  863.8 3.1 convolution_convert_fusion
  867.5 3.8 all-to-all-start.7
  871.4 2.8 fusion.20
  874.1 2.8 all-to-all-done.7
  878.7 6.1 convolution_add_fusion
  884.8 6.1 copy.150
  890.8 4.9 copy.152
  895.7 6.0 copy.151
  901.7 6.0 copy.153
  907.8 5.5 pad_maximum_fusion
  913.3 2.8 pad_maximum_fusion.1
  917.0 13.0 %all_gather.20 = bf16[128,2560]{0,1:T(8,128)(2,1)S(1)} all-gather(bf16[128,160]{0,1:T(8,128)(2,1)S(1)} %add_convert_fusion.2), channel_id=1, replica_groups=mesh['tp'=16] {'tp'}, dimensions={1}, use_global_device_ids=true | all-gather | bytes 696320 | tf_op jit(solution)/shard_map/all_gather | solution.py:77
  930.7 9.1 reduce-scatter.17.cloned.1.call-done
  940.7 13.3 %all_gather.23 = bf16[128,2560]{0,1:T(8,128)(2,1)S(1)} all-gather(bf16[128,160]{0,1:T(8,128)(2,1)S(1)} %add_convert_fusion), channel_id=1, replica_groups=mesh['tp'=16] {'tp'}, dimensions={1}, use_global_device_ids=true | all-gather | bytes 696320 | tf_op jit(solution)/shard_map/all_gather | solution.py:77
  954.7 10.6 %fusion.12 = f32[1,128,3200]{2,1,0:T(8,128)S(1)} fusion(bf16[3200,2560]{1,0:T(8,128)(2,1)} %param.17, bf16[128,2560]{0,1:T(8,128)(2,1)S(1)} %all_gather.20, f32[2560]{0:T(1024)S(1)} %copy-done.27, f32[128]{0:T(128)S(1)} %add_rsqrt_fusion.3, f32[128]{0:T(128)S(1)} %broadcast_multiply_fusion.3), kind=kOutput, calls=%fused_computation.58 | convolution fusion | flops 2099200000 | bytes 18689024 | tf_op jit(solution)/shard_map/dot_general | solution.py:79
  965.3 11.8 %fusion.13 = f32[1,128,3200]{2,1,0:T(8,128)} fusion(bf16[3200,2560]{1,0:T(8,128)(2,1)} %param.17, bf16[128,2560]{0,1:T(8,128)(2,1)S(1)} %all_gather.23, f32[128]{0:T(128)S(1)} %add_rsqrt_fusion, f32[128]{0:T(128)S(1)} %broadcast_multiply_fusion, f32[2560]{0:T(1024)S(1)} %copy-done.27), kind=kOutput, calls=%fused_computation.59 | convolution fusion | flops 2099200000 | bytes 18689024 | tf_op jit(solution)/shard_map/dot_general | solution.py:79
  977.1 3.3 pad_maximum_fusion.2
  (517 shorter events, 566.3 us)
Async XLA Ops:
  7.2 69.9 %reduce-scatter.13.cloned.1.call-start = ((), (), s32[]{:S(2)}) async-start(), calls=%async_computation.17 | async-start | bytes 696320 | tf_op jit(solution)/shard_map/reduce_scatter | solution.py:52
  19.4 113.1 %reduce-scatter.7.cloned.1.call-start = ((), (), s32[]{:S(2)}) async-start(), calls=%async_computation.14 | async-start | bytes 696320 | tf_op jit(solution)/shard_map/reduce_scatter | solution.py:52
  28.9 1.3 copy-start.36
  28.9 1.4 copy-start.28
  28.9 1.6 copy-start.12
  30.3 126.0 %copy-start.31 = (f32[8]{0:T(128)}, f32[8]{0:T(128)S(1)}, u32[]{:S(2)}) copy-start(f32[8]{0:T(128)S(1)} %get-tuple-element.298) | copy-start | bytes 100
  30.3 126.0 %copy-start.33 = (f32[8]{0:T(128)}, f32[8]{0:T(128)S(1)}, u32[]{:S(2)}) copy-start(f32[8]{0:T(128)S(1)} %get-tuple-element.299) | copy-start | bytes 100
  30.5 324.2 %copy-start.22 = (pred[8,2048]{1,0:T(8,128)(4,1)}, pred[8,2048]{1,0:T(8,128)(4,1)S(1)}, u32[]{:S(2)}) copy-start(pred[8,2048]{1,0:T(8,128)(4,1)S(1)} %get-tuple-element.311) | copy-start | bytes 49156
  30.5 424.2 %copy-start.20 = (pred[8,2048]{1,0:T(8,128)(4,1)}, pred[8,2048]{1,0:T(8,128)(4,1)S(1)}, u32[]{:S(2)}) copy-start(pred[8,2048]{1,0:T(8,128)(4,1)S(1)} %get-tuple-element.310) | copy-start | bytes 49156
  30.5 6.5 slice-start
  31.8 5.3 slice-start.1
  37.1 3.1 copy-start.35
  40.3 116.1 %copy-start.29 = (f32[40]{0:T(128)}, f32[40]{0:T(128)S(1)}, u32[]{:S(2)}) copy-start(f32[40]{0:T(128)S(1)} %multiply_power_fusion) | copy-start | bytes 484
  52.4 100.3 %copy-start.14 = (f32[128,40]{0,1:T(8,128)}, f32[128,40]{0,1:T(8,128)S(1)}, u32[]{:S(2)}) copy-start(f32[128,40]{0,1:T(8,128)S(1)} %get-tuple-element.302) | copy-start | bytes 61444
  52.4 100.3 %copy-start.16 = (f32[128,40]{0,1:T(8,128)}, f32[128,40]{0,1:T(8,128)S(1)}, u32[]{:S(2)}) copy-start(f32[128,40]{0,1:T(8,128)S(1)} %get-tuple-element.303) | copy-start | bytes 61444
  145.6 1.4 copy-start.6
  146.8 2.1 copy-start.8
  146.8 2.5 copy-start.10
  146.8 1.7 copy-start.4
  149.3 7.3 copy-start.13
  154.1 200.6 %all-to-all-start = ((bf16[128,2,80]{2,1,0:T(2,128)(2,1)}), bf16[128,2,80]{2,1,0:T(2,128)(2,1)S(1)}, u32[]{:S(2)}, u32[]{:S(2)}) async-start(bf16[128,2,80]{2,1,0:T(2,128)(2,1)} %copy.102), calls=%async_computation.1 | async-start | bytes 131072 | tf_op jit(solution)/shard_map/all_to_all | solution.py:64
  358.5 1.3 copy-start.1
  360.3 8.9 copy-start.24
  364.7 15.7 %copy-start.11 = (bf16[128,2560]{0,1:T(8,128)(2,1)S(1)}, bf16[128,2560]{0,1:T(8,128)(2,1)}, u32[]{:S(2)}) copy-start(bf16[128,2560]{0,1:T(8,128)(2,1)} %copy-done.10) | copy-start | bytes 1966084
  365.3 9.5 all-to-all-start.1
  374.8 79.9 %all-to-all-start.4 = ((bf16[128,2,80]{2,1,0:T(2,128)(2,1)}), bf16[128,2,80]{2,1,0:T(2,128)(2,1)S(1)}, u32[]{:S(2)}, u32[]{:S(2)}) async-start(bf16[128,2,80]{2,1,0:T(2,128)(2,1)} %copy.129), calls=%async_computation.8 | async-start | bytes 131072 | tf_op jit(solution)/shard_map/all_to_all | solution.py:64
  377.0 116.7 %reduce-scatter.9.cloned.1.call-start = ((), (), s32[]{:S(2)}) async-start(), calls=%async_computation.15 | async-start | bytes 1392640 | tf_op jit(solution)/shard_map/reduce_scatter | solution.py:75
  458.5 1.3 copy-start.2
  460.2 8.9 copy-start.9
  465.3 9.3 all-to-all-start.5
  469.1 70.1 %reduce-scatter.15.cloned.1.call-start = ((), (), s32[]{:S(2)}) async-start(), calls=%async_computation.18 | async-start | bytes 1392640 | tf_op jit(solution)/shard_map/reduce_scatter | solution.py:75
  487.8 6.0 copy-start.19
  493.7 45.5 %copy-start.18 = (bf16[128,160]{0,1:T(8,128)(2,1)S(1)}, bf16[128,160]{0,1:T(8,128)(2,1)}, u32[]{:S(2)}) copy-start(bf16[128,160]{0,1:T(8,128)(2,1)} %reduce-scatter.13.cloned.1.call-done) | copy-start | bytes 122884
  553.3 1.4 copy-start.7
  554.5 1.7 copy-start.3
  557.0 3.5 copy-start.30
  557.0 3.5 copy-start.32
  557.0 3.5 copy-start.34
  557.0 70.2 %copy-start.15 = (f32[128,40]{0,1:T(8,128)S(1)}, f32[128,40]{0,1:T(8,128)}, u32[]{:S(2)}) copy-start(f32[128,40]{0,1:T(8,128)} %copy-done.14) | copy-start | bytes 61444
  557.0 70.2 %copy-start.17 = (f32[128,40]{0,1:T(8,128)S(1)}, f32[128,40]{0,1:T(8,128)}, u32[]{:S(2)}) copy-start(f32[128,40]{0,1:T(8,128)} %copy-done.16) | copy-start | bytes 61444
  628.6 134.2 %all-to-all-start.2 = ((bf16[128,2,80]{2,1,0:T(2,128)(2,1)}), bf16[128,2,80]{2,1,0:T(2,128)(2,1)S(1)}, u32[]{:S(2)}, u32[]{:S(2)}) async-start(bf16[128,2,80]{2,1,0:T(2,128)(2,1)} %copy.115), calls=%async_computation.4 | async-start | bytes 131072 | tf_op jit(solution)/shard_map/all_to_all | solution.py:64
  630.9 132.1 %copy-start.23 = (pred[8,2048]{1,0:T(8,128)(4,1)S(1)}, pred[8,2048]{1,0:T(8,128)(4,1)}, u32[]{:S(2)}) copy-start(pred[8,2048]{1,0:T(8,128)(4,1)} %copy-done.22) | copy-start | bytes 49156
  767.2 9.0 copy-start.25
  767.2 9.0 copy-start.26
  770.9 15.2 %copy-start.37 = (f32[128,640]{1,0:T(8,128)S(1)}, f32[128,640]{1,0:T(8,128)}, u32[]{:S(2)}) copy-start(f32[128,640]{1,0:T(8,128)} %fusion.22) | copy-start | bytes 983044
  772.4 9.3 all-to-all-start.3
  781.8 77.7 %all-to-all-start.6 = ((bf16[128,2,80]{2,1,0:T(2,128)(2,1)}), bf16[128,2,80]{2,1,0:T(2,128)(2,1)S(1)}, u32[]{:S(2)}, u32[]{:S(2)}) async-start(bf16[128,2,80]{2,1,0:T(2,128)(2,1)} %copy.140), calls=%async_computation.11 | async-start | bytes 131072 | tf_op jit(solution)/shard_map/all_to_all | solution.py:64
  784.0 132.1 %reduce-scatter.11.cloned.1.call-start = ((), (), s32[]{:S(2)}) async-start(), calls=%async_computation.16 | async-start | bytes 1392640 | tf_op jit(solution)/shard_map/reduce_scatter | solution.py:75
  786.1 73.5 %copy-start.21 = (pred[8,2048]{1,0:T(8,128)(4,1)S(1)}, pred[8,2048]{1,0:T(8,128)(4,1)}, u32[]{:S(2)}) copy-start(pred[8,2048]{1,0:T(8,128)(4,1)} %copy-done.20) | copy-start | bytes 49156
  867.5 9.4 all-to-all-start.7
  871.3 5.6 copy-start.5
  871.3 68.5 %reduce-scatter.17.cloned.1.call-start = ((), (), s32[]{:S(2)}) async-start(), calls=%async_computation.19 | async-start | bytes 1392640 | tf_op jit(solution)/shard_map/reduce_scatter | solution.py:75
  907.8 5.5 copy-start
  917.0 37.7 %copy-start.27 = (f32[2560]{0:T(1024)S(1)}, f32[2560]{0:T(1024)}, u32[]{:S(2)}) copy-start(f32[2560]{0:T(1024)} %param.25) | copy-start | bytes 30724
Sparse Core Ops, SparseCore 0:
  19.6 57.4 reduce-scatter.12
  79.3 53.1 reduce-scatter.6
  386.7 57.2 reduce-scatter.8
  483.8 55.3 reduce-scatter.14
  792.0 57.3 reduce-scatter.10
  884.9 54.8 reduce-scatter.16
where the time goes:
time: 1010 us; the launch traced here: 988 us
  other arithmetic  351 us (35%)
  local copies, waits for them, and re-layouts  293 us (29%)
  waiting for transfers between devices  120 us (12%)
  matrix products  104 us (10%)
  blocking collectives  79.3 us (8%)
  starting transfers between devices  24.8 us (2%)
  between operations  15.3 us (2%)
    scatter x128, other arithmetic  323 us
    scatter x192, local copies, waits for them, and re-layouts  200 us
    all_gather x6, blocking collectives, device_fn(): full_resid = lax.all_gather(residual, 'tp', axis=1, tiled=True)  79.3 us
    reduce_scatter x2, waiting for transfers between devices, device_fn(): residual = lax.psum_scatter(emb_rows, 'tp', scatter_dimension=1, tiled=True)  66.5 us
    reduce_scatter x4, waiting for transfers between devices, device_fn(): lax.psum_scatter(attn_part + mlp_part, 'tp', scatter_dimension=1, tiled=T...  39.1 us
    unnamed x87, local copies, waits for them, and re-layouts  34.1 us
    dot_general x4, matrix products, device_fn(): jnp.dot(hidden, w_down[layer_idx], preferred_element_type=jnp.float32)  24.2 us
    scatter x4, local copies, waits for them, and re-layouts, write_rows(): lax.dynamic_update_slice(seq_cache, new_row[None], (at_pos, 0))  23 us
  transfers between devices with their start and end apart: 14, of which 8 were waited for; matrix products, arithmetic and copies ran while one was open for 61% of the time, Pallas kernels for 0%

commit v1 on v0

v1 whole, which is shorter than its diff:
```python
import functools

import jax
import jax.numpy as jnp
from jax import lax
from jax.experimental import pallas as pl
from jax.experimental.pallas import tpu as pltpu
from jax.sharding import PartitionSpec as P

LN_EPS = 1e-6
F32 = jnp.float32
BF16 = jnp.bfloat16


def layer_norm(residual, ln_gain):
    x_f32 = residual.astype(F32)
    row_mean = jnp.mean(x_f32, axis=-1, keepdims=True)
    centred = x_f32 - row_mean
    row_var = jnp.mean(centred * centred, axis=-1, keepdims=True)
    return (centred * lax.rsqrt(row_var + LN_EPS) * ln_gain).astype(BF16)


def attn_kernel(layer, has_alias, steps, seqs, len_ref, q_ref, kn_ref, vn_ref, kc_ref, vc_ref, *rest):
    if has_alias:
        rest = rest[2:]
    o_ref, ko_ref, vo_ref, kbuf, vbuf, qa, qb, oa, ob, isem, osem = rest
    head_dim, seq_len = kbuf.shape[1], kbuf.shape[2]
    rows_per = steps * seqs
    srcs = q_ref.shape[0] // rows_per
    width2 = q_ref.shape[1]

    def in_copies(s):
        return (pltpu.make_async_copy(kc_ref.at[layer, s], kbuf.at[s], isem.at[0, s]),
                pltpu.make_async_copy(vc_ref.at[layer, s], vbuf.at[s], isem.at[1, s]))

    def out_copies(s):
        return (pltpu.make_async_copy(kbuf.at[s], ko_ref.at[layer, s], osem.at[0, s]),
                pltpu.make_async_copy(vbuf.at[s], vo_ref.at[layer, s], osem.at[1, s]))

    for s in range(seqs):
        for cp in in_copies(s):
            cp.start()
    qa[...] = q_ref[:, :128].astype(F32)
    qb[...] = jnp.zeros_like(qb)
    qb[:, :width2 - 128] = q_ref[:, 128:].astype(F32)
    lane = lax.broadcasted_iota(jnp.int32, (head_dim, 128), 1)
    for s in range(seqs):
        for cp in in_copies(s):
            cp.wait()
        for t in range(steps):
            p = len_ref[s] + t
            base = pl.multiple_of((p // 128) * 128, 128)
            hit = lane == (p - base)
            c = t * seqs + s
            for buf, new in ((kbuf, kn_ref), (vbuf, vn_ref)):
                tile = buf[s, :, pl.ds(base, 128)].astype(F32)
                buf[s, :, pl.ds(base, 128)] = jnp.where(hit, new[:, c:c + 1], tile).astype(BF16)
        for cp in out_copies(s):
            cp.start()

    half = lax.broadcasted_iota(jnp.int32, (steps * srcs, width2), 1) < head_dim
    n_rows = 2 * steps * srcs
    scale = head_dim ** -0.5

    def attend(s, width):
        p = len_ref[s]
        at = [pl.ds(t * seqs + s, srcs, stride=rows_per) for t in range(steps)]
        qcat = jnp.concatenate([jnp.concatenate([qa[i, :], qb[i, :]], axis=1)[:, :width2] for i in at], axis=0)
        q2 = jnp.concatenate([jnp.where(half, qcat, 0.0), jnp.where(half, 0.0, qcat)], axis=0).astype(BF16)
        k = kbuf[s, :, 0:width]
        k2 = jnp.concatenate([k, k], axis=0)
        sc = jnp.dot(q2, k2, preferred_element_type=F32) * scale
        row = lax.broadcasted_iota(jnp.int32, (n_rows, width), 0)
        col = lax.broadcasted_iota(jnp.int32, (n_rows, width), 1)
        lim = p + lax.rem(row // srcs, steps)
        sc = jnp.where(col <= lim, sc, -jnp.inf)
        m = jnp.max(sc, axis=-1, keepdims=True)
        e = jnp.exp(sc - m)
        w = (e / jnp.sum(e, axis=-1, keepdims=True)).astype(BF16)
        v = vbuf[s, :, 0:width]
        v2 = jnp.concatenate([v, v], axis=0)
        o2 = lax.dot_general(w, v2, (((1,), (1,)), ((), ())), preferred_element_type=F32)
        o = jnp.where(half, o2[:n_rows // 2], o2[n_rows // 2:])
        o = jnp.concatenate([o, jnp.zeros((steps * srcs, 256 - width2), F32)], axis=1)
        for t in range(steps):
            oa[at[t], :] = o[t * srcs:(t + 1) * srcs, :128]
            ob[at[t], :] = o[t * srcs:(t + 1) * srcs, 128:]

    widths = [w for w in (256, 512, 1024) if w < seq_len] + [seq_len]

    @pl.loop(0, seqs)
    def _(s):
        last = len_ref[s] + (steps - 1)
        lo = 0
        for w in widths:
            @pl.when((last >= lo) & (last < w))
            def _():
                attend(s, w)
            lo = w

    o_ref[:, :128] = oa[...].astype(BF16)
    o_ref[:, 128:] = ob[:, :width2 - 128].astype(BF16)
    for s in range(seqs):
        for cp in out_copies(s):
            cp.wait()


def attention(layer, steps, local_len, q, k_new, v_new, kc, vc, outs):
    layers, seqs, head_dim, seq_len = kc.shape
    rows, width = q.shape
    any_spec = pl.BlockSpec(memory_space=pl.ANY)
    vm = pl.BlockSpec(memory_space=pltpu.VMEM)
    args = [local_len, q, k_new, v_new, kc, vc]
    in_specs = [pl.BlockSpec(memory_space=pltpu.SMEM), vm, vm, vm, any_spec, any_spec]
    aliases = {}
    if outs is not None:
        args += list(outs)
        in_specs += [any_spec, any_spec]
        aliases = {6: 1, 7: 2}
    return pl.pallas_call(
        functools.partial(attn_kernel, layer, outs is not None, steps, seqs),
        out_shape=(jax.ShapeDtypeStruct((rows, width), BF16), jax.ShapeDtypeStruct(kc.shape, BF16), jax.ShapeDtypeStruct(vc.shape, BF16)),
        in_specs=in_specs,
        out_specs=(vm, any_spec, any_spec),
        scratch_shapes=[
            pltpu.VMEM((seqs, head_dim, seq_len), BF16),
            pltpu.VMEM((seqs, head_dim, seq_len), BF16),
            pltpu.VMEM((rows, 128), F32),
            pltpu.VMEM((rows, 128), F32),
            pltpu.VMEM((rows, 128), F32),
            pltpu.VMEM((rows, 128), F32),
            pltpu.SemaphoreType.DMA((2, seqs)),
            pltpu.SemaphoreType.DMA((2, seqs)),
        ],
        input_output_aliases=aliases,
        compiler_params=pltpu.CompilerParams(vmem_limit_bytes=24 << 20),
        cost_estimate=pl.CostEstimate(flops=2_000_000_000, bytes_accessed=21 << 20, transcendentals=1 << 20),
        name=f"attend{layer}",
    )(*args)


def solution(mesh):
    n_dev = mesh.size

    def device_fn(tokens, lengths, embedding, ln_scale, w_q, w_kv, w_o, w_gate, w_up, w_down, final_scale, k_cache, v_cache):
        rank = lax.axis_index('tp')
        steps, batch = tokens.shape
        vocab_local, dim = embedding.shape
        layers, seqs, seq_len, head_dim = k_cache.shape
        heads_local = w_q.shape[2]
        width = heads_local * head_dim
        rows = steps * batch
        half = head_dim // 2
        kc = jnp.swapaxes(k_cache, 2, 3)
        vc = jnp.swapaxes(v_cache, 2, 3)
        local_len = lax.dynamic_slice_in_dim(lengths, rank * seqs, seqs)

        def by_device(per_step):
            return per_step.reshape(steps, n_dev, seqs).transpose(1, 0, 2).reshape(rows)

        tok = by_device(tokens)
        positions = by_device(lengths[None, :] + jnp.arange(steps, dtype=jnp.int32)[:, None])
        inv_freq = 10000.0 ** (-jnp.arange(half, dtype=F32) / half)
        ang = positions[:, None].astype(F32) * inv_freq
        cos_t = jnp.cos(ang)
        sin_t = jnp.sin(ang)
        cos_q = jnp.tile(cos_t, (1, 2 * heads_local))
        sin_q = jnp.tile(jnp.concatenate([-sin_t, sin_t], axis=1), (1, heads_local))
        local_rows = steps * seqs
        cos_k = lax.dynamic_slice_in_dim(cos_t, rank * local_rows, local_rows).T
        sin_k = lax.dynamic_slice_in_dim(sin_t, rank * local_rows, local_rows).T

        onehot = (tok[:, None] - rank * vocab_local == jnp.arange(vocab_local, dtype=jnp.int32)[None, :]).astype(BF16)
        emb = jnp.dot(onehot, embedding, preferred_element_type=F32).astype(BF16)
        x = lax.psum_scatter(emb, 'tp', scatter_dimension=0, tiled=True)
        outs = None
        for l in range(layers):
            h_local = layer_norm(x, ln_scale[l])
            h = lax.all_gather(h_local, 'tp', axis=0, tiled=True)
            q = jnp.dot(h, w_q[l].reshape(dim, width), preferred_element_type=F32)
            q4 = q.reshape(rows, heads_local, 2, half)
            q_sw = q4[:, :, ::-1].reshape(rows, width)
            q = (q * cos_q + q_sw * sin_q).astype(BF16)
            kv = lax.dot_general(w_kv[l], h_local, (((0,), (1,)), ((), ())), preferred_element_type=F32)
            k_lo, k_hi, v_new = kv[:half], kv[half:head_dim], kv[head_dim:]
            k_new = jnp.concatenate([k_lo * cos_k - k_hi * sin_k, k_lo * sin_k + k_hi * cos_k], axis=0)
            k_new = lax.reduce_precision(k_new, 8, 7)
            v_new = lax.reduce_precision(v_new, 8, 7)
            q_seq = lax.all_to_all(q, 'tp', 0, 0, tiled=True)
            o, *outs = attention(l, steps, local_len, q_seq, k_new, v_new, kc, vc, outs)
            gate = jnp.dot(h, w_gate[l], preferred_element_type=F32)
            up = jnp.dot(h, w_up[l], preferred_element_type=F32)
            hidden = (jax.nn.silu(gate) * up).astype(BF16)
            mlp = jnp.dot(hidden, w_down[l], preferred_element_type=F32)
            o_heads = lax.all_to_all(o, 'tp', 0, 0, tiled=True)
            part = jnp.dot(o_heads, w_o[l].reshape(width, dim), preferred_element_type=F32) + mlp
            total = lax.psum_scatter(part, 'tp', scatter_dimension=0, tiled=True)
            x = (x.astype(F32) + total).astype(BF16)
        h_local = layer_norm(x, final_scale)
        h = lax.all_gather(h_local, 'tp', axis=0, tiled=True)
        logits = lax.dot_general(h, embedding, (((1,), (1,)), ((), ())), preferred_element_type=F32) * dim ** -0.5
        logits = logits.reshape(n_dev, steps, seqs, vocab_local).transpose(1, 0, 2, 3).reshape(steps, batch, vocab_local)
        k_out, v_out = outs
        return logits, jnp.swapaxes(k_out, 2, 3), jnp.swapaxes(v_out, 2, 3)

    cache_spec = P(None, 'tp', None, None)
    in_specs = (P(), P(), P('tp', None), P(), P(None, None, 'tp', None), P(), P(None, 'tp', None, None), P(None, None, 'tp'), P(None, None, 'tp'), P(None, 'tp', None), P(), cache_spec, cache_spec)
    out_specs = (P(None, None, 'tp'), cache_spec, cache_spec)
    return jax.shard_map(device_fn, mesh=mesh, in_specs=in_specs, out_specs=out_specs, check_vma=False)
```

time: 1010 us -> 381 us (0.38); the launches traced: 988 us -> 380 us
  other arithmetic: 351 us -> 11.8 us
  local copies, waits for them, and re-layouts: 293 us -> 18.3 us
  waiting for transfers between devices: 120 us -> 259 us
  blocking collectives: 79.3 us -> 0 us
  matrix products: 104 us -> 50.5 us
  Pallas kernels: 0 us -> 15.5 us
  starting transfers between devices: 24.8 us -> 9.89 us
    scatter x129 -> x0, other arithmetic: 323 us -> none
    scatter x196 -> x0, local copies, waits for them, and re-layouts: 223 us -> none
    all_gather x6 -> x0, blocking collectives: 79.3 us -> none  [device_fn(): full_resid = lax.all_gather(residual, 'tp', axis=1, tiled=True)]
    all_gather x0 -> x3, waiting for transfers between devices: none -> 69.3 us  [device_fn(): h = lax.all_gather(h_local, 'tp', axis=0, tiled=True)]
    reduce_scatter x6 -> x3, waiting for transfers between devices: 106 us -> 174 us  [the longest x2 116 us: device_fn(): total = lax.psum_scatter(part, 'tp', scatter_dimension=0, tiled=True)]
    dot_general x26 -> x12, matrix products: 102 us -> 50.5 us  [the longest x2 15.1 us: device_fn(): mlp = jnp.dot(hidden, w_down[l], preferred_element_type=F32)]
    unnamed x87 -> x36, local copies, waits for them, and re-layouts: 34.1 us -> 10.7 us
    gather x4 -> x0, local copies, waits for them, and re-layouts: 19.4 us -> none  [device_fn(): jnp.take(embedding, jnp.clip(tok_local, 0, vocab_local - 1), axis=0)]
  transfers between devices with their start and end apart: 14 -> 10, of which waited for: 8 -> 10; matrix products, arithmetic and copies ran while one was open for 61% -> 4% of each run, Pallas kernels for 0% -> 0%
where the time goes in v1:
time: 381 us; the launch traced here: 380 us
  waiting for transfers between devices  259 us (68%)
  matrix products  50.5 us (13%)
  local copies, waits for them, and re-layouts  18.3 us (5%)
  Pallas kernels  15.5 us (4%)
  between operations  14.4 us (4%)
  other arithmetic  11.8 us (3%)
  starting transfers between devices  9.89 us (3%)
    reduce_scatter x2, waiting for transfers between devices, device_fn(): total = lax.psum_scatter(part, 'tp', scatter_dimension=0, tiled=True)  116 us
    all_gather x3, waiting for transfers between devices, device_fn(): h = lax.all_gather(h_local, 'tp', axis=0, tiled=True)  69.3 us
    reduce_scatter x1, waiting for transfers between devices, device_fn(): x = lax.psum_scatter(emb, 'tp', scatter_dimension=0, tiled=True)  57.8 us
    pallas_call x2, Pallas kernels, attention(): pl.pallas_call(functools.partial(attn_kernel, layer, outs is not None, st...  15.5 us
    dot_general x2, matrix products, device_fn(): mlp = jnp.dot(hidden, w_down[l], preferred_element_type=F32)  15.1 us
    all_to_all x2, waiting for transfers between devices, device_fn(): q_seq = lax.all_to_all(q, 'tp', 0, 0, tiled=True)  11.4 us
    unnamed x36, local copies, waits for them, and re-layouts  10.7 us
    dot_general x1, matrix products, device_fn(): emb = jnp.dot(onehot, embedding, preferred_element_type=F32).astype(BF16)  9.89 us
  transfers between devices with their start and end apart: 10, of which 10 were waited for; matrix products, arithmetic and copies ran while one was open for 4% of the time, Pallas kernels for 0%

profile of v1, /device:TPU:0, one launch (start us, length us, event | category | flops | bytes accessed | tf_op | source)
XLA Modules:
  0.0 379.7 jit_solution(11928315240973706056)
XLA Ops:
  7.2 0.7 broadcast_subtract_fusion
  7.9 0.1 sub.52
  8.0 0.1 sub.54
  8.1 9.9 %convolution_convert_fusion = bf16[256,2560]{1,0:T(8,128)(2,1)} fusion(bf16[3200,2560]{1,0:T(8,128)(2,1)} %param.15, s32[256]{0:T(256)S(1)} %sub.54), kind=kOutput, calls=%fused_computation.3 | convolution fusion | flops 4195778560 | bytes 17695744 | tf_op jit(solution)/shard_map/dot_general | solution.py:174
  18.0 0.0 all-gather.4.cloned.1.call-start
  18.1 0.1 add.91
  18.2 0.1 dynamic_slice.9.len_ref
  18.3 0.1 convert_element_type.57
  18.4 0.6 slice_reduce_fusion
  19.0 57.8 %reduce-scatter.4.cloned.1.call-done = bf16[16,2560]{1,0:T(8,128)(2,1)} async-done(((bf16[256,2560]{1,0:T(8,128)(2,1)}), bf16[16,2560]{1,0:T(8,128)(2,1)}) %reduce-scatter.4.cloned.1.call-update) | async-done | bytes 81936 | tf_op jit(solution)/shard_map/reduce_scatter | solution.py:175
  76.8 1.0 convert_reduce_fusion.1
  77.9 1.1 fusion.58
  79.0 1.6 fusion.60
  80.6 0.2 multiply_cosine_fusion
  80.8 0.6 pad_maximum_fusion
  81.5 1.6 fusion.80
  83.1 1.5 fusion.79
  84.7 0.3 convolution_bitcast_fusion.1
  85.0 0.7 fusion.70
  85.7 19.6 %all-gather.4.cloned.1.call-done = bf16[256,2560]{1,0:T(8,128)(2,1)} async-done(((bf16[16,2560]{1,0:T(8,128)(2,1)}), bf16[256,2560]{1,0:T(8,128)(2,1)}) %all-gather.4.cloned.1.call-update) | async-done | bytes 1310736 | tf_op jit(solution)/shard_map/all_gather | solution.py:179
  105.3 1.9 fusion.81
  107.2 0.9 fusion.67
  108.2 0.8 copy.42
  108.9 2.5 all-to-all-start
  111.4 0.7 maximum_reduce-precision_fusion.kn_ref
  112.1 5.4 %all-to-all-done = bf16[16,16,160]{2,1,0:T(8,128)(2,1)S(1)} async-done(((bf16[16,16,160]{2,1,0:T(8,128)(2,1)}), bf16[16,16,160]{2,1,0:T(8,128)(2,1)S(1)}, u32[]{:S(2)}, u32[]{:S(2)}) %all-to-all-start) | async-done | bytes 81952 | tf_op jit(solution)/shard_map/all_to_all | solution.py:189
  117.5 2.5 copy-done
  120.0 2.5 copy-done.2
  122.5 7.8 %attend0.1 = (bf16[256,160]{1,0:T(8,128)(2,1)}, bf16[2,8,80,2048]{3,2,1,0:T(8,128)(2,1)}, bf16[2,8,80,2048]{3,2,1,0:T(8,128)(2,1)}) custom-call(s32[8]{0:T(128)S(1)} %dynamic_slice.9.len_ref, bf16[256,160]{1,0:T(8,128)(2,1)S(1)} %bitcast.135, f32[80,16]{1,0:T(8,128)S(1)} %maximum_reduce-precision_fusion.kn_ref, ...), custom_call_target="tpu_custom_call" | custom-call | flops 2000000000 | bytes 22020096 | tf_op jit(solution)/shard_map/attend0/pallas_call | solution.py:120
  130.2 2.3 all-to-all-start.1
  132.5 0.0 reduce-scatter.6.cloned.1.call-start
  132.6 3.5 fusion.8
  136.1 2.5 all-to-all-done.1
  138.6 2.0 fusion.82
  140.6 7.8 %convolution_add_fusion.1 = f32[256,2560]{1,0:T(8,128)} fusion(f32[256,2560]{1,0:T(8,128)} %fusion.82, bf16[2,640,2560]{2,1,0:T(8,128)(2,1)} %param.22, bf16[256,2560]{1,0:T(8,128)(2,1)} %all-gather.4.cloned.1.call-done, bf16[2,2560,640]{2,1,0:T(8,128)(2,1)} %param.21, f32[256,640]{1,0:T(8,128)S(1)} %fusion.8), kind=kOutput, calls=%fused_computation.2 | convolution fusion | flops 1679360000 | bytes 13762560 | tf_op jit(solution)/shard_map/dot_general | solution.py:194
  148.4 0.0 all-gather.6.cloned.1.call-start
  148.5 57.4 %reduce-scatter.6.cloned.1.call-done = f32[16,2560]{1,0:T(8,128)} async-done(((f32[256,2560]{1,0:T(8,128)}), f32[16,2560]{1,0:T(8,128)}) %reduce-scatter.6.cloned.1.call-update) | async-done | bytes 163856 | tf_op jit(solution)/shard_map/reduce_scatter | solution.py:197
  205.8 1.1 convert_reduce_fusion
  206.9 0.2 fusion.55
  207.1 0.7 fusion.57
  207.9 1.5 convolution_bitcast_fusion
  209.4 0.1 fusion.72
  209.5 24.3 %all-gather.6.cloned.1.call-done = bf16[256,2560]{1,0:T(8,128)(2,1)} async-done(((bf16[16,2560]{1,0:T(8,128)(2,1)}), bf16[256,2560]{1,0:T(8,128)(2,1)}) %all-gather.6.cloned.1.call-update) | async-done | bytes 1310736 | tf_op jit(solution)/shard_map/all_gather | solution.py:179
  233.8 1.9 fusion.83
  235.8 0.8 copy.44
  236.5 2.5 all-to-all-start.2
  239.0 6.1 %all-to-all-done.2 = bf16[16,16,160]{2,1,0:T(8,128)(2,1)S(1)} async-done(((bf16[16,16,160]{2,1,0:T(8,128)(2,1)}), bf16[16,16,160]{2,1,0:T(8,128)(2,1)S(1)}, u32[]{:S(2)}, u32[]{:S(2)}) %all-to-all-start.2) | async-done | bytes 81952 | tf_op jit(solution)/shard_map/all_to_all | solution.py:189
  245.1 2.5 copy-done.1
  247.6 2.5 copy-done.3
  250.1 7.8 %attend1.1 = (bf16[256,160]{1,0:T(8,128)(2,1)}, bf16[2,8,80,2048]{3,2,1,0:T(8,128)(2,1)}, bf16[2,8,80,2048]{3,2,1,0:T(8,128)(2,1)}) custom-call(s32[8]{0:T(128)S(1)} %dynamic_slice.9.len_ref, bf16[256,160]{1,0:T(8,128)(2,1)S(1)} %bitcast.134, f32[80,16]{1,0:T(8,128)S(1)} %maximum_reduce-precision_fusion.1.kn_ref, ...), custom_call_target="tpu_custom_call", output_to_operand_aliasing={{1}: (6, {}), {2}: (7, {})} | custom-call | flops 2000000000 | bytes 22020096 | tf_op jit(solution)/shard_map/attend1/pallas_call | solution.py:120
  257.8 2.4 all-to-all-start.3
  260.3 4.0 %fusion.3 = f32[256,640]{1,0:T(8,128)} fusion(bf16[256,2560]{1,0:T(8,128)(2,1)S(1)} %copy-done.4, bf16[2,2560,640]{2,1,0:T(8,128)(2,1)} %param.20), kind=kOutput, calls=%fused_computation.7 | convolution fusion | flops 838860800 | bytes 5242880 | tf_op jit(solution)/shard_map/dot_general | solution.py:191
  264.3 2.0 all-to-all-done.3
  266.3 0.7 copy-done.9
  267.0 1.4 fusion.84
  268.4 7.3 %convolution_add_fusion = f32[256,2560]{1,0:T(8,128)} fusion(f32[256,2560]{1,0:T(8,128)S(1)} %fusion.84, bf16[2,640,2560]{2,1,0:T(8,128)(2,1)} %param.22, bf16[256,2560]{1,0:T(8,128)(2,1)} %all-gather.6.cloned.1.call-done, bf16[2,2560,640]{2,1,0:T(8,128)(2,1)} %param.21, f32[256,640]{1,0:T(8,128)} %fusion.3), kind=kOutput, calls=%fused_computation.1 | convolution fusion | flops 1679360000 | bytes 13762560 | tf_op jit(solution)/shard_map/dot_general | solution.py:194
  275.7 0.0 all-gather.8.cloned.1.call-start
  275.7 58.7 %reduce-scatter.8.cloned.1.call-done = f32[16,2560]{1,0:T(8,128)} async-done(((f32[256,2560]{1,0:T(8,128)}), f32[16,2560]{1,0:T(8,128)}) %reduce-scatter.8.cloned.1.call-update) | async-done | bytes 163856 | tf_op jit(solution)/shard_map/reduce_scatter | solution.py:197
  334.4 1.1 convert_reduce_fusion.2
  335.5 0.2 fusion.61
  335.7 0.7 fusion.63
  336.5 25.4 %all-gather.8.cloned.1.call-done = bf16[256,2560]{1,0:T(8,128)(2,1)} async-done(((bf16[16,2560]{1,0:T(8,128)(2,1)}), bf16[256,2560]{1,0:T(8,128)(2,1)}) %all-gather.8.cloned.1.call-update) | async-done | bytes 1310736 | tf_op jit(solution)/shard_map/all_gather | solution.py:200
  361.9 9.0 %convolution_multiply_fusion = f32[256,3200]{1,0:T(8,128)S(1)} fusion(bf16[256,2560]{1,0:T(8,128)(2,1)} %all-gather.8.cloned.1.call-done, bf16[3200,2560]{1,0:T(8,128)(2,1)} %param.15), kind=kOutput, calls=%fused_computation | convolution fusion | flops 4195123200 | bytes 20971520 | tf_op jit(solution)/shard_map/dot_general | solution.py:201
  370.9 1.9 copy.50
  (54 shorter events, 0.4 us)
Async XLA Ops:
  7.2 69.7 %reduce-scatter.4.cloned.1.call-start = ((), (), s32[]{:S(2)}) async-start(), calls=%async_computation.7 | async-start | bytes 1392640 | tf_op jit(solution)/shard_map/reduce_scatter | solution.py:175
  8.1 10.0 %copy-start.16 = (s32[128]{0:T(128)S(1)}, s32[128]{0:T(128)}, u32[]{:S(2)}) copy-start(s32[128]{0:T(128)} %param.14) | copy-start | bytes 1540
  8.1 10.3 %copy-start.14 = (f32[2,2560]{1,0:T(2,128)S(1)}, f32[2,2560]{1,0:T(2,128)}, u32[]{:S(2)}) copy-start(f32[2,2560]{1,0:T(2,128)} %param.16) | copy-start | bytes 61444
  18.0 87.3 %all-gather.4.cloned.1.call-start = ((), (), s32[]{:S(2)}) async-start(), calls=%async_computation.8 | async-start | bytes 1392640 | tf_op jit(solution)/shard_map/all_gather | solution.py:179
  80.8 4.2 %copy-start.10 = (f32[256,40]{0,1:T(8,128)}, f32[256,40]{0,1:T(8,128)S(1)}, u32[]{:S(2)}) copy-start(f32[256,40]{0,1:T(8,128)S(1)} %get-tuple-element.31) | copy-start | bytes 122884
  80.8 26.4 %copy-start.7 = (f32[256,40]{0,1:T(8,128)}, f32[256,40]{0,1:T(8,128)S(1)}, u32[]{:S(2)}) copy-start(f32[256,40]{0,1:T(8,128)S(1)} %get-tuple-element.29) | copy-start | bytes 122884
  81.5 3.2 copy-start.12
  81.5 3.2 copy-start.17
  108.9 8.6 %all-to-all-start = ((bf16[16,16,160]{2,1,0:T(8,128)(2,1)}), bf16[16,16,160]{2,1,0:T(8,128)(2,1)S(1)}, u32[]{:S(2)}, u32[]{:S(2)}) async-start(bf16[16,16,160]{2,1,0:T(8,128)(2,1)} %bitcast.6), calls=%async_computation.1 | async-start | bytes 262144 | tf_op jit(solution)/shard_map/all_to_all | solution.py:189
  117.5 2.5 copy-start
  120.0 2.5 copy-start.2
  130.2 8.3 %all-to-all-start.1 = ((bf16[16,16,160]{2,1,0:T(8,128)(2,1)}), bf16[16,16,160]{2,1,0:T(8,128)(2,1)S(1)}, u32[]{:S(2)}, u32[]{:S(2)}) async-start(bf16[16,16,160]{2,1,0:T(8,128)(2,1)} %bitcast.14), calls=%async_computation.2 | async-start | bytes 262144 | tf_op jit(solution)/shard_map/all_to_all | solution.py:195
  132.5 73.3 %reduce-scatter.6.cloned.1.call-start = ((), (), s32[]{:S(2)}) async-start(), calls=%async_computation.9 | async-start | bytes 2785280 | tf_op jit(solution)/shard_map/reduce_scatter | solution.py:197
  148.4 57.5 %copy-start.5 = (bf16[16,2560]{1,0:T(8,128)(2,1)S(1)}, bf16[16,2560]{1,0:T(8,128)(2,1)}, u32[]{:S(2)}) copy-start(bf16[16,2560]{1,0:T(8,128)(2,1)} %reduce-scatter.4.cloned.1.call-done) | copy-start | bytes 245764
  148.4 58.7 %copy-start.13 = (f32[2560]{0:T(1024)S(1)}, f32[2560]{0:T(1024)}, u32[]{:S(2)}) copy-start(f32[2560]{0:T(1024)} %get-tuple-element.15) | copy-start | bytes 30724
  148.4 61.0 %copy-start.8 = (f32[256,40]{0,1:T(8,128)S(1)}, f32[256,40]{0,1:T(8,128)}, u32[]{:S(2)}) copy-start(f32[256,40]{0,1:T(8,128)} %copy-done.7) | copy-start | bytes 122884
  148.4 61.0 %copy-start.11 = (f32[256,40]{0,1:T(8,128)S(1)}, f32[256,40]{0,1:T(8,128)}, u32[]{:S(2)}) copy-start(f32[256,40]{0,1:T(8,128)} %copy-done.10) | copy-start | bytes 122884
  148.4 87.3 %copy-start.6 = (f32[256,80]{0,1:T(8,128)S(1)}, f32[256,80]{0,1:T(8,128)}, u32[]{:S(2)}) copy-start(f32[256,80]{0,1:T(8,128)} %pad_maximum_fusion) | copy-start | bytes 245764
  148.4 85.4 %all-gather.6.cloned.1.call-start = ((), (), s32[]{:S(2)}) async-start(), calls=%async_computation.10 | async-start | bytes 1392640 | tf_op jit(solution)/shard_map/all_gather | solution.py:179
  236.5 8.6 %all-to-all-start.2 = ((bf16[16,16,160]{2,1,0:T(8,128)(2,1)}), bf16[16,16,160]{2,1,0:T(8,128)(2,1)S(1)}, u32[]{:S(2)}, u32[]{:S(2)}) async-start(bf16[16,16,160]{2,1,0:T(8,128)(2,1)} %bitcast.23), calls=%async_computation.4 | async-start | bytes 262144 | tf_op jit(solution)/shard_map/all_to_all | solution.py:189
  245.1 2.5 copy-start.1
  247.6 2.5 copy-start.3
  250.1 10.3 %copy-start.4 = (bf16[256,2560]{1,0:T(8,128)(2,1)S(1)}, bf16[256,2560]{1,0:T(8,128)(2,1)}, u32[]{:S(2)}) copy-start(bf16[256,2560]{1,0:T(8,128)(2,1)} %all-gather.6.cloned.1.call-done) | copy-start | bytes 3932164
  257.8 8.5 %all-to-all-start.3 = ((bf16[16,16,160]{2,1,0:T(8,128)(2,1)}), bf16[16,16,160]{2,1,0:T(8,128)(2,1)S(1)}, u32[]{:S(2)}, u32[]{:S(2)}) async-start(bf16[16,16,160]{2,1,0:T(8,128)(2,1)} %bitcast.27), calls=%async_computation.5 | async-start | bytes 262144 | tf_op jit(solution)/shard_map/all_to_all | solution.py:195
  260.3 74.2 %reduce-scatter.8.cloned.1.call-start = ((), (), s32[]{:S(2)}) async-start(), calls=%async_computation.11 | async-start | bytes 2785280 | tf_op jit(solution)/shard_map/reduce_scatter | solution.py:197
  266.3 0.7 copy-start.9
  275.6 60.1 %copy-start.15 = (f32[2560]{0:T(1024)S(1)}, f32[2560]{0:T(1024)}, u32[]{:S(2)}) copy-start(f32[2560]{0:T(1024)} %param.23) | copy-start | bytes 30724
  275.7 86.2 %all-gather.8.cloned.1.call-start = ((), (), s32[]{:S(2)}) async-start(), calls=%async_computation.12 | async-start | bytes 1392640 | tf_op jit(solution)/shard_map/all_gather | solution.py:200
Sparse Core Ops, SparseCore 0:
  18.2 58.6 reduce-scatter.3
  80.7 24.5 all-gather.3
  148.5 57.2 reduce-scatter.5
  208.5 25.2 all-gather.5
  275.8 58.5 reduce-scatter.7
  337.1 24.7 all-gather.7

commit v2 on v1

--- a/solution.py
+++ b/solution.py
@@ -10,14 +10,6 @@
 LN_EPS = 1e-6
 F32 = jnp.float32
 BF16 = jnp.bfloat16
-
-
-def layer_norm(residual, ln_gain):
-    x_f32 = residual.astype(F32)
-    row_mean = jnp.mean(x_f32, axis=-1, keepdims=True)
-    centred = x_f32 - row_mean
-    row_var = jnp.mean(centred * centred, axis=-1, keepdims=True)
-    return (centred * lax.rsqrt(row_var + LN_EPS) * ln_gain).astype(BF16)
 
 
 def attn_kernel(layer, has_alias, steps, seqs, len_ref, q_ref, kn_ref, vn_ref, kc_ref, vc_ref, *rest):
@@ -108,7 +100,7 @@
 def attention(layer, steps, local_len, q, k_new, v_new, kc, vc, outs):
     layers, seqs, head_dim, seq_len = kc.shape
     rows, width = q.shape
-    any_spec = pl.BlockSpec(memory_space=pl.ANY)
+    any_spec = pl.BlockSpec(memory_space=pltpu.HBM)
     vm = pl.BlockSpec(memory_space=pltpu.VMEM)
     args = [local_len, q, k_new, v_new, kc, vc]
     in_specs = [pl.BlockSpec(memory_space=pltpu.SMEM), vm, vm, vm, any_spec, any_spec]
@@ -139,6 +131,226 @@
     )(*args)
 
 
+def device(d):
+    return {"device_id": (d,), "device_id_type": pl.DeviceIdType.MESH}
+
+
+def enter(n_dev, me):
+    sem = pltpu.get_barrier_semaphore()
+    for i in range(1, n_dev):
+        pl.semaphore_signal(sem, inc=1, **device(lax.rem(me + i, n_dev)))
+    return sem
+
+
+def chip_at(chip, j, n_bits):
+    total = 0
+    for i in range(n_bits):
+        total = total + lax.rem(chip // (1 << i) + ((j >> i) & 1), 2) * (1 << i)
+    return total
+
+
+def block(d, rows):
+    return pl.ds(pl.multiple_of(d * rows, rows), rows)
+
+
+def norm_rows(x_f32, gain):
+    row_mean = jnp.mean(x_f32, axis=-1, keepdims=True)
+    centred = x_f32 - row_mean
+    row_var = jnp.mean(centred * centred, axis=-1, keepdims=True)
+    return (centred * lax.rsqrt(row_var + LN_EPS) * gain).astype(BF16)
+
+
+def reduce_gather(n_dev, me, part, x_ref, gain, x_out, h_out, hloc, d2d, stage, rem, sems, while_gathering):
+    d2d_s, d2d_r, far_s, far_r, ag_s, ag_r, fw_s, fw_r = sems
+    n_chips = n_dev // 2
+    n_bits = n_chips.bit_length() - 1
+    rows = hloc.shape[0]
+    chip, core = me // 2, lax.rem(me, 2)
+    sibling = chip * 2 + 1 - core
+    order = sorted(range(n_chips), key=lambda j: -bin(j).count("1"))
+
+    def pre(j):
+        c = chip_at(chip, j, n_bits)
+        return pltpu.make_async_remote_copy(part.at[block(c * 2 + 1 - core, rows)], d2d.at[j], d2d_s.at[j], d2d_r.at[j], **device(sibling))
+
+    def far(j):
+        c = chip_at(chip, j, n_bits)
+        return pltpu.make_async_remote_copy(stage.at[j], rem.at[j], far_s.at[j], far_r.at[j], **device(c * 2 + core))
+
+    for j in order:
+        pre(j).start()
+    for j in order[:-1]:
+        pre(j).wait_recv()
+        c = chip_at(chip, j, n_bits)
+        stage[j] = (part[block(c * 2 + core, rows)].astype(F32) + d2d[j].astype(F32)).astype(stage.dtype)
+        far(j).start()
+    pre(0).wait_recv()
+    acc = part[block(me, rows)].astype(F32) + d2d[0].astype(F32)
+    for j in reversed(order[:-1]):
+        far(j).wait_recv()
+        acc = acc + rem[j].astype(F32)
+    if x_ref is not None:
+        acc = x_ref[...].astype(F32) + acc
+    x_new = acc.astype(BF16)
+    x_out[...] = x_new
+    hloc[...] = norm_rows(x_new.astype(F32), gain)
+    h_out[block(me, rows)] = hloc[...]
+
+    def gather(j):
+        c = chip_at(chip, j, n_bits)
+        return pltpu.make_async_remote_copy(hloc, h_out.at[block(me, rows)], ag_s.at[j], ag_r.at[j], **device(c * 2 + core if j else sibling))
+
+    def relay(j):
+        c = chip_at(chip, j, n_bits)
+        blk = h_out.at[block(c * 2 + core, rows)]
+        return pltpu.make_async_remote_copy(blk, blk, fw_s.at[j], fw_r.at[j], **device(sibling))
+
+    for j in order:
+        gather(j).start()
+    while_gathering()
+    for j in reversed(order[:-1]):
+        gather(j).wait_recv()
+        relay(j).start()
+    gather(0).wait_recv()
+    for j in order[:-1]:
+        relay(j).wait_recv()
+    for j in order:
+        pre(j).wait_send()
+        gather(j).wait_send()
+        if j:
+            far(j).wait_send()
+            relay(j).wait_send()
+
+
+def project_kv(hloc, wkv_ref, cos_ref, sin_ref, kn_ref, vn_ref):
+    head_dim = kn_ref.shape[0]
+    half = head_dim // 2
+    kv = lax.dot_general(wkv_ref[...], hloc[...], (((1,), (1,)), ((), ())), preferred_element_type=F32)
+    k_lo, k_hi = kv[:half], kv[half:head_dim]
+    cos, sin = cos_ref[...], sin_ref[...]
+    kn_ref[...] = jnp.concatenate([k_lo * cos - k_hi * sin, k_lo * sin + k_hi * cos], axis=0).astype(BF16).astype(F32)
+    vn_ref[...] = kv[head_dim:].astype(BF16).astype(F32)
+
+
+def reduce_scratch(n_dev, rows, dim, dtype):
+    n_chips = n_dev // 2
+    return [pltpu.VMEM((rows, dim), BF16)] + [pltpu.VMEM((n_chips, rows, dim), dtype)] * 3 + [pltpu.SemaphoreType.DMA((n_chips,))] * 8
+
+
+def boundary_kernel(n_dev, kind, last, *refs):
+    refs = list(refs)
+    take = lambda n: [refs.pop(0) for _ in range(n)]
+    if kind == "embed":
+        part_in, gain = take(2)
+        x_ref = None
+    else:
+        o_ref, wo_ref, mlp_ref, x_ref, gain = take(5)
+    if not last:
+        wkv_ref, cos_ref, sin_ref = take(3)
+    x_out, h_out = take(2)
+    if not last:
+        kn_ref, vn_ref = take(2)
+    if kind == "embed":
+        part = part_in
+    else:
+        heads, part, a2a_s, a2a_r = take(4)
+    hloc, d2d, stage, rem, *sems = refs
+    me = lax.axis_index("tp")
+    bar = enter(n_dev, me)
+    pl.semaphore_wait(bar, n_dev - 1)
+    rows = hloc.shape[0]
+    if kind != "embed":
+        def send(i):
+            d = lax.rem(me + i, n_dev)
+            return pltpu.make_async_remote_copy(o_ref.at[block(d, rows)], heads.at[block(me, rows)], a2a_s.at[i], a2a_r.at[i], **device(d))
+        for i in range(1, n_dev):
+            send(i).start()
+        heads[block(me, rows)] = o_ref[block(me, rows)]
+        for i in range(1, n_dev):
+            send(i).wait_recv()
+        part[...] = jnp.dot(heads[...], wo_ref[...], preferred_element_type=F32) + mlp_ref[...]
+    body = (lambda: None) if last else (lambda: project_kv(hloc, wkv_ref, cos_ref, sin_ref, kn_ref, vn_ref))
+    reduce_gather(n_dev, me, part, x_ref, gain[...], x_out, h_out, hloc, d2d, stage, rem, sems, body)
+    if kind != "embed":
+        for i in range(1, n_dev):
+            send(i).wait_send()
+
+
+def boundary(n_dev, kind, index, ins, gain, kv_ins, rows_total):
+    vm = pl.BlockSpec(memory_space=pltpu.VMEM)
+    dim = gain.shape[1]
+    rows = rows_total // n_dev
+    last = kv_ins is None
+    args = list(ins) + [gain] + ([] if last else list(kv_ins))
+    out_shape = [jax.ShapeDtypeStruct((rows, dim), BF16), jax.ShapeDtypeStruct((rows_total, dim), BF16)]
+    if not last:
+        head_dim = kv_ins[0].shape[0] // 2
+        out_shape += [jax.ShapeDtypeStruct((head_dim, rows), F32)] * 2
+    scratch = []
+    if kind != "embed":
+        width = ins[0].shape[1]
+        scratch = [pltpu.VMEM((rows_total, width), BF16), pltpu.VMEM((rows_total, dim), F32), pltpu.SemaphoreType.DMA((n_dev,)), pltpu.SemaphoreType.DMA((n_dev,))]
+    scratch += reduce_scratch(n_dev, rows, dim, BF16 if kind == "embed" else F32)
+    return pl.pallas_call(
+        functools.partial(boundary_kernel, n_dev, kind, last),
+        out_shape=tuple(out_shape),
+        in_specs=[vm] * len(args),
+        out_specs=tuple([vm] * len(out_shape)),
+        scratch_shapes=scratch,
+        compiler_params=pltpu.CompilerParams(vmem_limit_bytes=24 << 20, collective_id=index, has_side_effects=True),
+        cost_estimate=pl.CostEstimate(flops=20_000_000_000, bytes_accessed=8 << 20, transcendentals=0),
+        name=f"boundary{index}",
+    )(*args)
+
+
+def project_kernel(n_dev, h_ref, wq_ref, cos_ref, sin_ref, wg_ref, wu_ref, wd_ref, q_out, mlp_ref, q_buf, hid, s_sem, r_sem):
+    me = lax.axis_index("tp")
+    bar = enter(n_dev, me)
+    rows = q_buf.shape[0] // n_dev
+    half = cos_ref.shape[0]
+    h = h_ref[...]
+    qt = lax.dot_general(wq_ref[...], h, (((1,), (1,)), ((), ())), preferred_element_type=F32)
+    cos, sin = cos_ref[...], sin_ref[...]
+    parts = []
+    for a in range(0, qt.shape[0], 2 * half):
+        lo, hi = qt[a:a + half], qt[a + half:a + 2 * half]
+        parts += [lo * cos - hi * sin, lo * sin + hi * cos]
+    q_buf[...] = jnp.concatenate(parts, axis=0).T.astype(BF16)
+    pl.semaphore_wait(bar, n_dev - 1)
+
+    def send(i):
+        d = lax.rem(me + i, n_dev)
+        return pltpu.make_async_remote_copy(q_buf.at[block(d, rows)], q_out.at[block(me, rows)], s_sem.at[i], r_sem.at[i], **device(d))
+
+    for i in range(1, n_dev):
+        send(i).start()
+    q_out[block(me, rows)] = q_buf[block(me, rows)]
+    gate = jnp.dot(h, wg_ref[...], preferred_element_type=F32)
+    up = jnp.dot(h, wu_ref[...], preferred_element_type=F32)
+    hid[...] = (gate * jax.nn.sigmoid(gate) * up).astype(BF16)
+    mlp_ref[...] = jnp.dot(hid[...], wd_ref[...], preferred_element_type=F32)
+    for i in range(1, n_dev):
+        send(i).wait_recv()
+    for i in range(1, n_dev):
+        send(i).wait_send()
+
+
+def project(n_dev, index, h, wq_t, cos_t, sin_t, wg, wu, wd):
+    vm = pl.BlockSpec(memory_space=pltpu.VMEM)
+    rows, dim = h.shape
+    width = wq_t.shape[0]
+    return pl.pallas_call(
+        functools.partial(project_kernel, n_dev),
+        out_shape=(jax.ShapeDtypeStruct((rows, width), BF16), jax.ShapeDtypeStruct((rows, dim), F32)),
+        in_specs=[vm] * 7,
+        out_specs=(vm, vm),
+        scratch_shapes=[pltpu.VMEM((rows, width), BF16), pltpu.VMEM((rows, wg.shape[1]), BF16), pltpu.SemaphoreType.DMA((n_dev,)), pltpu.SemaphoreType.DMA((n_dev,))],
+        compiler_params=pltpu.CompilerParams(vmem_limit_bytes=28 << 20, collective_id=index, has_side_effects=True),
+        cost_estimate=pl.CostEstimate(flops=6_000_000_000, bytes_accessed=14 << 20, transcendentals=0),
+        name=f"project{index}",
+    )(h, wq_t, cos_t, sin_t, wg, wu, wd)
+
+
 def solution(mesh):
     n_dev = mesh.size
 
@@ -161,43 +373,27 @@
         tok = by_device(tokens)
         positions = by_device(lengths[None, :] + jnp.arange(steps, dtype=jnp.int32)[:, None])
         inv_freq = 10000.0 ** (-jnp.arange(half, dtype=F32) / half)
-        ang = positions[:, None].astype(F32) * inv_freq
+        ang = inv_freq[:, None] * positions[None, :].astype(F32)
         cos_t = jnp.cos(ang)
         sin_t = jnp.sin(ang)
-        cos_q = jnp.tile(cos_t, (1, 2 * heads_local))
-        sin_q = jnp.tile(jnp.concatenate([-sin_t, sin_t], axis=1), (1, heads_local))
         local_rows = steps * seqs
-        cos_k = lax.dynamic_slice_in_dim(cos_t, rank * local_rows, local_rows).T
-        sin_k = lax.dynamic_slice_in_dim(sin_t, rank * local_rows, local_rows).T
+        cos_k = lax.dynamic_slice_in_dim(cos_t, rank * local_rows, local_rows, axis=1)
+        sin_k = lax.dynamic_slice_in_dim(sin_t, rank * local_rows, local_rows, axis=1)
+        wq_t = jnp.moveaxis(w_q, 1, 3).reshape(layers, width, dim)
+        wkv_t = jnp.swapaxes(w_kv, 1, 2)
+        gains = [ln_scale[l][None] for l in range(layers)] + [final_scale[None]]
 
         onehot = (tok[:, None] - rank * vocab_local == jnp.arange(vocab_local, dtype=jnp.int32)[None, :]).astype(BF16)
         emb = jnp.dot(onehot, embedding, preferred_element_type=F32).astype(BF16)
-        x = lax.psum_scatter(emb, 'tp', scatter_dimension=0, tiled=True)
+        x, h, k_new, v_new = boundary(n_dev, "embed", 0, (emb,), gains[0], (wkv_t[0], cos_k, sin_k), rows)
         outs = None
         for l in range(layers):
-            h_local = layer_norm(x, ln_scale[l])
-            h = lax.all_gather(h_local, 'tp', axis=0, tiled=True)
-            q = jnp.dot(h, w_q[l].reshape(dim, width), preferred_element_type=F32)
-            q4 = q.reshape(rows, heads_local, 2, half)
-            q_sw = q4[:, :, ::-1].reshape(rows, width)
-            q = (q * cos_q + q_sw * sin_q).astype(BF16)
-            kv = lax.dot_general(w_kv[l], h_local, (((0,), (1,)), ((), ())), preferred_element_type=F32)
-            k_lo, k_hi, v_new = kv[:half], kv[half:head_dim], kv[head_dim:]
-            k_new = jnp.concatenate([k_lo * cos_k - k_hi * sin_k, k_lo * sin_k + k_hi * cos_k], axis=0)
-            k_new = lax.reduce_precision(k_new, 8, 7)
-            v_new = lax.reduce_precision(v_new, 8, 7)
-            q_seq = lax.all_to_all(q, 'tp', 0, 0, tiled=True)
+            q_seq, mlp = project(n_dev, 1 + 2 * l, h, wq_t[l], cos_t, sin_t, w_gate[l], w_up[l], w_down[l])
             o, *outs = attention(l, steps, local_len, q_seq, k_new, v_new, kc, vc, outs)
-            gate = jnp.dot(h, w_gate[l], preferred_element_type=F32)
-            up = jnp.dot(h, w_up[l], preferred_element_type=F32)
-            hidden = (jax.nn.silu(gate) * up).astype(BF16)
-            mlp = jnp.dot(hidden, w_down[l], preferred_element_type=F32)
-            o_heads = lax.all_to_all(o, 'tp', 0, 0, tiled=True)
-            part = jnp.dot(o_heads, w_o[l].reshape(width, dim), preferred_element_type=F32) + mlp
-            total = lax.psum_scatter(part, 'tp', scatter_dimension=0, tiled=True)
-            x = (x.astype(F32) + total).astype(BF16)
-        h_local = layer_norm(x, final_scale)
-        h = lax.all_gather(h_local, 'tp', axis=0, tiled=True)
+            kv_ins = (wkv_t[l + 1], cos_k, sin_k) if l + 1 < layers else None
+            x, h, *kv = boundary(n_dev, "layer", 2 + 2 * l, (o, w_o[l].reshape(width, dim), mlp, x), gains[l + 1], kv_ins, rows)
+            if kv:
+                k_new, v_new = kv
         logits = lax.dot_general(h, embedding, (((1,), (1,)), ((), ())), preferred_element_type=F32) * dim ** -0.5
         logits = logits.reshape(n_dev, steps, seqs, vocab_local).transpose(1, 0, 2, 3).reshape(steps, batch, vocab_local)
         k_out, v_out = outs

time: 381 us -> 182 us (0.48)
  waiting for transfers between devices: 259 us -> 0 us
  Pallas kernels: 15.5 us -> 134 us
  matrix products: 50.5 us -> 19.1 us
  between operations: 14.4 us -> 0.99 us
  other arithmetic: 11.8 us -> 0.95 us
  starting transfers between devices: 9.89 us -> 0 us
  local copies, waits for them, and re-layouts: 18.3 us -> 27.1 us
    reduce_scatter x3 -> x0, waiting for transfers between devices: 174 us -> none  [the longest x2 116 us: device_fn(): total = lax.psum_scatter(part, 'tp', scatter_dimension=0, tiled=True)]
    pallas_call x0 -> x5, Pallas kernels: none -> 119 us  [the longest x3 107 us: boundary(): pl.pallas_call(functools.partial(boundary_kernel, n_dev, kind, last), out...]
    all_gather x3 -> x0, waiting for transfers between devices: 69.3 us -> none  [device_fn(): h = lax.all_gather(h_local, 'tp', axis=0, tiled=True)]
    dot_general x10 -> x0, matrix products: 31.6 us -> none  [the longest x2 15.1 us: device_fn(): mlp = jnp.dot(hidden, w_down[l], preferred_element_type=F32)]
    all_to_all x4 -> x0, waiting for transfers between devices: 15.9 us -> none  [the longest x2 11.4 us: device_fn(): q_seq = lax.all_to_all(q, 'tp', 0, 0, tiled=True)]
    squeeze x0 -> x3, local copies, waits for them, and re-layouts: none -> 10.8 us  [the longest x1 5.13 us: device_fn(): w_down[l]]
    all_to_all x4 -> x0, starting transfers between devices: 9.65 us -> none  [the longest x2 4.93 us: device_fn(): q_seq = lax.all_to_all(q, 'tp', 0, 0, tiled=True)]
    reduce_sum x6 -> x0, other arithmetic: 4.63 us -> none  [the longest x3 3.12 us: layer_norm(): row_mean = jnp.mean(x_f32, axis=-1, keepdims=True)]
  transfers between devices with their start and end apart: 10 -> 0, of which waited for: 10 -> 0; matrix products, arithmetic and copies ran while one was open for 4% -> 0% of each run, Pallas kernels for 0% -> 0%
where the time goes in v2:
time: 182 us
  Pallas kernels  134 us (74%)
  local copies, waits for them, and re-layouts  27.1 us (15%)
  matrix products  19.1 us (10%)
    pallas_call x3, Pallas kernels, boundary(): pl.pallas_call(functools.partial(boundary_kernel, n_dev, kind, last), out...  107 us
    pallas_call x2, Pallas kernels, attention(): pl.pallas_call(functools.partial(attn_kernel, layer, outs is not None, st...  14.6 us
    pallas_call x2, Pallas kernels, project(): pl.pallas_call(functools.partial(project_kernel, n_dev), out_shape=(jax.S...  12 us
    dot_general x1, matrix products, device_fn(): lax.dot_general(h, embedding, (((1,), (1,)), ((), ())), preferred_element...  10.2 us
    unnamed x54, local copies, waits for them, and re-layouts  9.56 us
    dot_general x1, matrix products, device_fn(): emb = jnp.dot(onehot, embedding, preferred_element_type=F32).astype(BF16)  8.97 us
    squeeze x1, local copies, waits for them, and re-layouts, device_fn(): w_down[l]  5.13 us
    squeeze x1, local copies, waits for them, and re-layouts, device_fn(): w_up[l]  4.65 us

profile of v2, /device:TPU:0, one launch (start us, length us, event | category | flops | bytes accessed | tf_op | source)
XLA Modules:
  0.0 182.1 jit_solution(16390362684018959867)
XLA Ops:
  0.6 0.7 add.29
  1.4 0.1 convert_element_type.17
  1.5 0.2 multiply_sine_fusion
  1.7 0.1 constant_dynamic-slice_fusion
  1.8 0.7 broadcast_subtract_fusion
  2.5 0.1 sub.22
  2.6 0.1 sub.24
  2.7 0.0 copy-start.15
  2.7 9.0 %convolution_convert_fusion.refs_0_ = bf16[256,2560]{1,0:T(8,128)(2,1)S(1)} fusion(bf16[3200,2560]{1,0:T(8,128)(2,1)} %param.15, s32[256]{0:T(256)S(1)} %sub.24), kind=kOutput, calls=%fused_computation.1 | convolution fusion | flops 4195778560 | bytes 17695744 | tf_op jit(solution)/shard_map/dot_general | solution.py:387
  11.7 0.0 copy-start.18
  11.7 0.0 copy-done.15
  11.7 0.0 slice-start.4
  11.7 1.0 slice_bitcast_fusion.6
  12.7 0.0 copy-done.18
  12.8 0.6 fusion.3
  13.4 0.0 copy-done.8
  13.4 27.8 %boundary0.1 = (bf16[16,2560]{1,0:T(8,128)(2,1)S(1)}, bf16[256,2560]{1,0:T(8,128)(2,1)S(1)}, f32[80,16]{1,0:T(8,128)S(1)}, f32[80,16]{1,0:T(8,128)S(1)}) custom-call(bf16[256,2560]{1,0:T(8,128)(2,1)S(1)} %convolution_convert_fusion.refs_0_, f32[1,2560]{1,0:T(1,128)S(1)} %get-tuple-element.54.refs_1_, bf16[160,2560]{1,0:T(8,128)(2,1)S(1)} %get-tuple-element.52.refs_2_, ...), custom_call_target="tpu_custom_call" | custom-call | flops 20000000000 | bytes 8388608 | tf_op jit(solution)/shard_map/boundary0/pallas_call | solution.py:294
  41.2 0.0 copy-start.6
  41.2 0.6 copy-done.6
  41.8 0.6 copy-done.13
  42.5 0.0 slice-done.4
  42.5 0.0 slice-done.5
  42.5 4.6 %slice_bitcast_fusion.1 = (bf16[2560,640]{1,0:T(8,128)(2,1)S(1)}, bf16[2560,640]{1,0:T(8,128)(2,1)S(1)}, bf16[2560,640]{1,0:T(8,128)(2,1)S(1)}, bf16[2560,640]{1,0:T(8,128)(2,1)}) fusion(bf16[2,2560,640]{2,1,0:T(8,128)(2,1)S(1)} %bitcast.49, bf16[2,2560,640]{2,1,0:T(8,128)(2,1)} %param.20), kind=kLoop, calls=%fused_computation.4 | loop fusion | bytes 26214400 | tf_op jit(solution)/shard_map/squeeze | solution.py:391
  47.1 5.1 %slice_bitcast_fusion = (bf16[640,2560]{1,0:T(8,128)(2,1)}, bf16[640,2560]{1,0:T(8,128)(2,1)S(1)}) fusion(bf16[2,640,2560]{2,1,0:T(8,128)(2,1)} %param.22), kind=kLoop, calls=%fused_computation.3 | loop fusion | bytes 13107200 | tf_op jit(solution)/shard_map/squeeze | solution.py:391
  52.3 0.0 copy-done.16
  52.3 1.0 fusion.2
  53.3 5.9 %project1.1 = (bf16[256,160]{1,0:T(8,128)(2,1)S(1)}, f32[256,2560]{1,0:T(8,128)S(1)}) custom-call(bf16[256,2560]{1,0:T(8,128)(2,1)S(1)} %get-tuple-element.22.h_ref, bf16[160,2560]{1,0:T(8,128)(2,1)S(1)} %bitcast.47, f32[40,256]{1,0:T(8,128)S(1)} %get-tuple-element.56.cos_ref, f32[40,256]{1,0:T(8,128)S(1)} %get-tuple-element.55.sin_ref, ...), custom_call_target="tpu_custom_call" | custom-call | flops 6000000000 | bytes 14680064 | tf_op jit(solution)/shard_map/project1/pallas_call | solution.py:342
  59.2 0.0 copy-start.11
  59.2 1.5 copy-done.11
  60.7 0.0 copy-done.20
  60.7 0.1 dynamic_slice.9.len_ref
  60.7 2.5 %copy-done = bf16[2,8,2048,80]{2,3,1,0:T(8,128)(2,1)S(1)} copy-done((bf16[2,8,2048,80]{2,3,1,0:T(8,128)(2,1)S(1)}, bf16[2,8,2048,80]{2,3,1,0:T(8,128)(2,1)}, u32[]{:S(2)}) %copy-start) | copy-done | bytes 5242904
  63.2 2.5 %copy-done.1 = bf16[2,8,2048,80]{2,3,1,0:T(8,128)(2,1)S(1)} copy-done((bf16[2,8,2048,80]{2,3,1,0:T(8,128)(2,1)S(1)}, bf16[2,8,2048,80]{2,3,1,0:T(8,128)(2,1)}, u32[]{:S(2)}) %copy-start.1) | copy-done | bytes 5242904
  65.7 0.8 copy-done.7
  66.5 7.4 %attend0.1 = (bf16[256,160]{1,0:T(8,128)(2,1)S(1)}, bf16[2,8,80,2048]{3,2,1,0:T(8,128)(2,1)}, bf16[2,8,80,2048]{3,2,1,0:T(8,128)(2,1)}) custom-call(s32[8]{0:T(128)S(1)} %dynamic_slice.9.len_ref, bf16[256,160]{1,0:T(8,128)(2,1)S(1)} %get-tuple-element.23.q_ref, f32[80,16]{1,0:T(8,128)S(1)} %get-tuple-element.24.kn_ref, f32[80,16]{1,0:T(8,128)S(1)} %copy-done.7, ...), custom_call_target="tpu_custom_call" | custom-call | flops 2000000000 | bytes 22020096 | tf_op jit(solution)/shard_map/attend0/pallas_call | solution.py:112
  73.9 0.0 copy-start.4
  73.9 0.0 copy-start.9
  73.9 0.0 copy-start.10
  73.9 0.0 copy-start.14
  74.0 0.0 copy-done.17
  74.0 0.1 fusion.1
  74.1 0.0 copy-done.12
  74.1 0.9 copy-done.4
  75.1 0.0 copy-done.9
  75.1 0.0 copy-done.10
  75.1 0.0 copy-done.14
  75.1 0.0 copy-start.5
  75.1 39.4 %boundary2.1 = (bf16[16,2560]{1,0:T(8,128)(2,1)S(1)}, bf16[256,2560]{1,0:T(8,128)(2,1)S(1)}, f32[80,16]{1,0:T(8,128)S(1)}, f32[80,16]{1,0:T(8,128)S(1)}) custom-call(bf16[256,160]{1,0:T(8,128)(2,1)S(1)} %get-tuple-element.26.refs_0_, bf16[160,2560]{1,0:T(8,128)(2,1)S(1)} %bitcast.46, f32[256,2560]{1,0:T(8,128)S(1)} %copy-done.12, ...), custom_call_target="tpu_custom_call" | custom-call | flops 20000000000 | bytes 8388608 | tf_op jit(solution)/shard_map/boundary2/pallas_call | solution.py:294
  114.5 0.0 slice-start
  114.5 0.0 slice-start.2
  114.5 0.0 copy-done.2
  114.5 0.0 copy-done.3
  114.6 0.0 copy-done.5
  114.6 0.0 slice-start.1
  114.6 0.0 slice-start.3
  114.6 6.2 %project3.1 = (bf16[256,160]{1,0:T(8,128)(2,1)S(1)}, f32[256,2560]{1,0:T(8,128)S(1)}) custom-call(bf16[256,2560]{1,0:T(8,128)(2,1)S(1)} %get-tuple-element.29.h_ref, bf16[160,2560]{1,0:T(8,128)(2,1)S(1)} %bitcast.44, f32[40,256]{1,0:T(8,128)S(1)} %get-tuple-element.56.cos_ref, f32[40,256]{1,0:T(8,128)S(1)} %get-tuple-element.55.sin_ref, ...), custom_call_target="tpu_custom_call" | custom-call | flops 6000000000 | bytes 14680064 | tf_op jit(solution)/shard_map/project3/pallas_call | solution.py:342
  120.8 0.0 slice-done
  120.8 0.0 slice-done.2
  120.8 0.0 slice-done.1
  120.8 0.0 copy-start.19
  120.8 7.2 %attend1.1 = (bf16[256,160]{1,0:T(8,128)(2,1)S(1)}, bf16[2,8,80,2048]{3,2,1,0:T(8,128)(2,1)}, bf16[2,8,80,2048]{3,2,1,0:T(8,128)(2,1)}) custom-call(s32[8]{0:T(128)S(1)} %dynamic_slice.9.len_ref, bf16[256,160]{1,0:T(8,128)(2,1)S(1)} %get-tuple-element.30.q_ref, f32[80,16]{1,0:T(8,128)S(1)} %get-tuple-element.31.kn_ref, ...), custom_call_target="tpu_custom_call", output_to_operand_aliasing={{1}: (6, {}), {2}: (7, {})} | custom-call | flops 2000000000 | bytes 22020096 | tf_op jit(solution)/shard_map/attend1/pallas_call | solution.py:112
  128.1 40.0 %boundary4.1 = (bf16[16,2560]{1,0:T(8,128)(2,1)}, bf16[256,2560]{1,0:T(8,128)(2,1)S(1)}) custom-call(bf16[256,160]{1,0:T(8,128)(2,1)S(1)} %get-tuple-element.35.refs_0_, bf16[160,2560]{1,0:T(8,128)(2,1)S(1)} %bitcast.45, f32[256,2560]{1,0:T(8,128)S(1)} %get-tuple-element.36.refs_2_, bf16[16,2560]{1,0:T(8,128)(2,1)S(1)} %get-tuple-element.37.refs_3_, ...), custom_call_target="tpu_custom_call" | custom-call | flops 20000000000 | bytes 8388608 | tf_op jit(solution)/shard_map/boundary4/pallas_call | solution.py:294
  168.1 10.2 %convolution_multiply_fusion = f32[256,3200]{1,0:T(8,128)} fusion(bf16[256,2560]{1,0:T(8,128)(2,1)S(1)} %get-tuple-element.38, bf16[3200,2560]{1,0:T(8,128)(2,1)} %param.15), kind=kOutput, calls=%fused_computation | convolution fusion | flops 4195123200 | bytes 20971520 | tf_op jit(solution)/shard_map/dot_general | solution.py:397
  178.3 3.8 %copy.22 = f32[2,16,8,3200]{3,2,1,0:T(8,128)} copy(f32[2,16,8,3200]{3,2,0,1:T(8,128)} %bitcast.53) | data formatting | bytes 6553600 | tf_op jit(solution)/shard_map/transpose | solution.py:398
  (21 shorter events, 0.1 us)
Async XLA Ops:
  1.8 11.6 %copy-start.8 = (f32[40,16]{1,0:T(8,128)}, f32[40,16]{1,0:T(8,128)S(1)}, u32[]{:S(2)}) copy-start(f32[40,16]{1,0:T(8,128)S(1)} %get-tuple-element.58.refs_3_.refs_6_) | copy-start | bytes 7684
  2.7 9.0 %copy-start.15 = (bf16[2,2560,160]{1,2,0:T(8,128)(2,1)S(1)}, bf16[2,2560,160]{1,2,0:T(8,128)(2,1)}, u32[]{:S(2)}) copy-start(bf16[2,2560,160]{1,2,0:T(8,128)(2,1)} %param.18) | copy-start | bytes 4915204
  11.7 1.0 copy-start.18
  11.7 30.7 %slice-start.4 = ((s8[6553600]{0:T(1024)(128)(4,1)}), s8[4194304]{0:T(1024)(128)(4,1)S(1)}, s32[]{:S(2)}) async-start(s8[6553600]{0:T(1024)(128)(4,1)} %bitcast.48), calls=%async_computation.4 | async-start | bytes 8388608
  13.4 29.1 %slice-start.5 = ((s8[6553600]{0:T(1024)(128)(4,1)}), s8[2359296]{0:T(1024)(128)(4,1)S(1)}, s32[]{:S(2)}) async-start(s8[6553600]{0:T(1024)(128)(4,1)} %bitcast.48), calls=%async_computation.5 | async-start | bytes 4718592
  41.2 0.6 copy-start.6
  41.8 0.6 copy-start.13
  47.1 5.1 %copy-start.16 = (bf16[2,2560,2,80]{1,3,2,0:T(8,128)(2,1)S(1)}, bf16[2,2560,2,80]{1,3,2,0:T(8,128)(2,1)}, u32[]{:S(2)}) copy-start(bf16[2,2560,2,80]{1,3,2,0:T(8,128)(2,1)} %param.17) | copy-start | bytes 4915204
  53.3 7.4 %copy-start.20 = (s32[128]{0:T(128)S(1)}, s32[128]{0:T(128)}, u32[]{:S(2)}) copy-start(s32[128]{0:T(128)} %param.14) | copy-start | bytes 1540
  59.2 1.5 copy-start.11
  60.7 2.5 %copy-start = (bf16[2,8,2048,80]{2,3,1,0:T(8,128)(2,1)S(1)}, bf16[2,8,2048,80]{2,3,1,0:T(8,128)(2,1)}, u32[]{:S(2)}) copy-start(bf16[2,8,2048,80]{2,3,1,0:T(8,128)(2,1)} %param.24) | copy-start | bytes 15728644
  63.2 2.5 %copy-start.1 = (bf16[2,8,2048,80]{2,3,1,0:T(8,128)(2,1)S(1)}, bf16[2,8,2048,80]{2,3,1,0:T(8,128)(2,1)}, u32[]{:S(2)}) copy-start(bf16[2,8,2048,80]{2,3,1,0:T(8,128)(2,1)} %param.25) | copy-start | bytes 15728644
  65.7 0.8 copy-start.7
  66.5 7.5 %copy-start.17 = (bf16[2,2,80,2560]{3,2,1,0:T(8,128)(2,1)S(1)}, bf16[2,2,80,2560]{3,2,1,0:T(8,128)(2,1)}, u32[]{:S(2)}) copy-start(bf16[2,2,80,2560]{3,2,1,0:T(8,128)(2,1)} %param.19) | copy-start | bytes 4915204
  66.5 7.6 %copy-start.12 = (f32[256,2560]{1,0:T(8,128)S(1)}, f32[256,2560]{1,0:T(8,128)}, u32[]{:S(2)}) copy-start(f32[256,2560]{1,0:T(8,128)} %copy-done.11) | copy-start | bytes 7864324
  73.9 1.1 copy-start.4
  73.9 1.1 copy-start.9
  73.9 1.1 copy-start.10
  73.9 1.1 copy-start.14
  75.1 39.5 %copy-start.2 = (bf16[2560,640]{1,0:T(8,128)(2,1)S(1)}, bf16[2560,640]{1,0:T(8,128)(2,1)}, u32[]{:S(2)}) copy-start(bf16[2560,640]{1,0:T(8,128)(2,1)} %get-tuple-element.60.wg_ref) | copy-start | bytes 9830404
  75.1 39.5 %copy-start.3 = (bf16[640,2560]{1,0:T(8,128)(2,1)S(1)}, bf16[640,2560]{1,0:T(8,128)(2,1)}, u32[]{:S(2)}) copy-start(bf16[640,2560]{1,0:T(8,128)(2,1)} %get-tuple-element.41.wd_ref) | copy-start | bytes 9830404
  75.1 39.5 %copy-start.5 = (bf16[1,2,80,2560]{3,2,1,0:T(8,128)(2,1)S(1)}, bf16[1,2,80,2560]{3,2,1,0:T(8,128)(2,1)}, u32[]{:S(2)}) copy-start(bf16[1,2,80,2560]{3,2,1,0:T(8,128)(2,1)} %get-tuple-element.49) | copy-start | bytes 2457604
  114.5 6.2 %slice-start = ((s8[5242880]{0:T(1024)(128)(4,1)}), s8[4194304]{0:T(1024)(128)(4,1)S(1)}, s32[]{:S(2)}) async-start(s8[5242880]{0:T(1024)(128)(4,1)} %bitcast.37), calls=%async_computation | async-start | bytes 8388608
  114.5 6.2 %slice-start.2 = ((s8[5242880]{0:T(1024)(128)(4,1)}), s8[4194304]{0:T(1024)(128)(4,1)S(1)}, s32[]{:S(2)}) async-start(s8[5242880]{0:T(1024)(128)(4,1)} %bitcast.41), calls=%async_computation.2 | async-start | bytes 8388608
  114.6 6.2 %slice-start.1 = ((s8[5242880]{0:T(1024)(128)(4,1)}), s8[1048576]{0:T(1024)(128)(4,1)S(1)}, s32[]{:S(2)}) async-start(s8[5242880]{0:T(1024)(128)(4,1)} %bitcast.37), calls=%async_computation.1 | async-start | bytes 2097152
  114.6 6.2 %slice-start.3 = ((s8[5242880]{0:T(1024)(128)(4,1)}), s8[1048576]{0:T(1024)(128)(4,1)S(1)}, s32[]{:S(2)}) async-start(s8[5242880]{0:T(1024)(128)(4,1)} %bitcast.41), calls=%async_computation.3 | async-start | bytes 2097152
  120.8 7.3 %copy-start.19 = (f32[2560]{0:T(1024)S(1)}, f32[2560]{0:T(1024)}, u32[]{:S(2)}) copy-start(f32[2560]{0:T(1024)} %param.23) | copy-start | bytes 30724

commit v3 on v2

--- a/solution.py
+++ b/solution.py
@@ -192,7 +192,8 @@
     if x_ref is not None:
         acc = x_ref[...].astype(F32) + acc
     x_new = acc.astype(BF16)
-    x_out[...] = x_new
+    if x_out is not None:
+        x_out[...] = x_new
     hloc[...] = norm_rows(x_new.astype(F32), gain)
     h_out[block(me, rows)] = hloc[...]
 
@@ -222,133 +223,205 @@
             relay(j).wait_send()
 
 
-def project_kv(hloc, wkv_ref, cos_ref, sin_ref, kn_ref, vn_ref):
-    head_dim = kn_ref.shape[0]
-    half = head_dim // 2
-    kv = lax.dot_general(wkv_ref[...], hloc[...], (((1,), (1,)), ((), ())), preferred_element_type=F32)
-    k_lo, k_hi = kv[:half], kv[half:head_dim]
-    cos, sin = cos_ref[...], sin_ref[...]
-    kn_ref[...] = jnp.concatenate([k_lo * cos - k_hi * sin, k_lo * sin + k_hi * cos], axis=0).astype(BF16).astype(F32)
-    vn_ref[...] = kv[head_dim:].astype(BF16).astype(F32)
-
-
 def reduce_scratch(n_dev, rows, dim, dtype):
     n_chips = n_dev // 2
     return [pltpu.VMEM((rows, dim), BF16)] + [pltpu.VMEM((n_chips, rows, dim), dtype)] * 3 + [pltpu.SemaphoreType.DMA((n_chips,))] * 8
 
 
-def boundary_kernel(n_dev, kind, last, *refs):
+def lookup_kernel(tok_ref, emb_ref, out_ref, buf, row32, out32, sem):
+    n_rows, group = buf.shape[0], buf.shape[1]
+    vocab = emb_ref.shape[0]
+
+    def fetch(i):
+        first = pl.multiple_of((tok_ref[i] // group) * group, group)
+        return pltpu.make_async_copy(emb_ref.at[pl.ds(first, group), :], buf.at[i], sem.at[i])
+
+    def each(fn):
+        @pl.loop(0, n_rows // 8)
+        def _(base):
+            for u in range(8):
+                i = base * 8 + u
+                tok = tok_ref[i]
+
+                @pl.when((tok >= 0) & (tok < vocab))
+                def _():
+                    fn(i, tok)
+
+    each(lambda i, tok: fetch(i).start())
+    out32[...] = jnp.zeros_like(out32)
+
+    def place(i, tok):
+        fetch(i).wait()
+        row32[...] = buf[i].astype(F32)
+        out32[pl.ds(i, 1), :] = row32[pl.ds(lax.rem(tok, group), 1), :]
+
+    each(place)
+    out_ref[...] = out32[...].astype(BF16)
+
+
+def lookup(tok, embedding):
+    rows, dim, group = tok.shape[0], embedding.shape[1], 16
+    return pl.pallas_call(
+        lookup_kernel,
+        out_shape=jax.ShapeDtypeStruct((rows, dim), BF16),
+        in_specs=[pl.BlockSpec(memory_space=pltpu.SMEM), pl.BlockSpec(memory_space=pltpu.HBM)],
+        out_specs=pl.BlockSpec(memory_space=pltpu.VMEM),
+        scratch_shapes=[pltpu.VMEM((rows, group, dim), BF16), pltpu.VMEM((group, dim), F32), pltpu.VMEM((rows, dim), F32), pltpu.SemaphoreType.DMA((rows,))],
+        compiler_params=pltpu.CompilerParams(vmem_limit_bytes=32 << 20),
+        cost_estimate=pl.CostEstimate(flops=1_000_000_000, bytes_accessed=2 << 20, transcendentals=0),
+        name="lookup",
+    )(tok, embedding)
+
+
+def logits_kernel(n_dev, seqs, scale, h_ref, e_ref, out_ref):
+    steps = out_ref.shape[0]
+    acc = lax.dot_general(h_ref[...], e_ref[...], (((1,), (1,)), ((), ())), preferred_element_type=F32) * scale
+    for d in range(n_dev):
+        for t in range(steps):
+            at = (d * steps + t) * seqs
+            out_ref[t, d * seqs:(d + 1) * seqs, :] = acc[at:at + seqs]
+
+
+def output_head(n_dev, steps, seqs, h, embedding):
+    rows, dim = h.shape
+    vocab = embedding.shape[0]
+    tile = 640
+    return pl.pallas_call(
+        functools.partial(logits_kernel, n_dev, seqs, dim ** -0.5),
+        grid=(vocab // tile,),
+        out_shape=jax.ShapeDtypeStruct((steps, rows // steps, vocab), F32),
+        in_specs=[pl.BlockSpec((rows, dim), lambda i: (0, 0)), pl.BlockSpec((tile, dim), lambda i: (i, 0))],
+        out_specs=pl.BlockSpec((steps, rows // steps, tile), lambda i: (0, 0, i)),
+        compiler_params=pltpu.CompilerParams(vmem_limit_bytes=28 << 20),
+        cost_estimate=pl.CostEstimate(flops=4_000_000_000, bytes_accessed=20 << 20, transcendentals=0),
+        name="head",
+    )(h, embedding)
+
+
+def layer_kernel(n_dev, layer, first, last, *refs):
     refs = list(refs)
     take = lambda n: [refs.pop(0) for _ in range(n)]
-    if kind == "embed":
-        part_in, gain = take(2)
+    if first:
+        part, gain = take(2)
         x_ref = None
     else:
-        o_ref, wo_ref, mlp_ref, x_ref, gain = take(5)
+        o_ref, hid_ref, x_ref, gain, wo_hbm, wd_hbm = take(6)
     if not last:
-        wkv_ref, cos_ref, sin_ref = take(3)
-    x_out, h_out = take(2)
+        cos_ref, sin_ref, cosk_ref, sink_ref, wkv_hbm, wq_hbm, wg_hbm, wu_hbm = take(8)
+        x_out, q_out, hid_out, kn_ref, vn_ref = take(5)
+    else:
+        (h_out,) = take(1)
+    hloc, d2d, stage, rem, *sems = take(12)
+    copies = []
+    if not first:
+        heads, part, wo, wd, a2a_s, a2a_r, w_sem = take(7)
+        copies += [pltpu.make_async_copy(wd_hbm.at[layer - 1], wd, w_sem.at[0]), pltpu.make_async_copy(wo_hbm.at[layer - 1], wo, w_sem.at[1])]
     if not last:
-        kn_ref, vn_ref = take(2)
-    if kind == "embed":
-        part = part_in
+        h_out, q_buf, wkv, wq, wg, wu, q_s, q_r, p_sem = take(9)
+        starts = [pltpu.make_async_copy(src.at[layer], dst, p_sem.at[i]) for i, (src, dst) in enumerate(((wkv_hbm, wkv), (wq_hbm, wq), (wg_hbm, wg), (wu_hbm, wu)))]
     else:
-        heads, part, a2a_s, a2a_r = take(4)
-    hloc, d2d, stage, rem, *sems = refs
+        starts = []
+        x_out = None
+    for cp in copies + starts:
+        cp.start()
     me = lax.axis_index("tp")
     bar = enter(n_dev, me)
     pl.semaphore_wait(bar, n_dev - 1)
     rows = hloc.shape[0]
-    if kind != "embed":
+
+    def exchange(src, dst, s_sem, r_sem):
         def send(i):
             d = lax.rem(me + i, n_dev)
-            return pltpu.make_async_remote_copy(o_ref.at[block(d, rows)], heads.at[block(me, rows)], a2a_s.at[i], a2a_r.at[i], **device(d))
-        for i in range(1, n_dev):
-            send(i).start()
+            return pltpu.make_async_remote_copy(src.at[block(d, rows)], dst.at[block(me, rows)], s_sem.at[i], r_sem.at[i], **device(d))
+        return [send(i) for i in range(1, n_dev)]
+
+    if not first:
+        sends = exchange(o_ref, heads, a2a_s, a2a_r)
+        for cp in sends:
+            cp.start()
         heads[block(me, rows)] = o_ref[block(me, rows)]
-        for i in range(1, n_dev):
-            send(i).wait_recv()
-        part[...] = jnp.dot(heads[...], wo_ref[...], preferred_element_type=F32) + mlp_ref[...]
-    body = (lambda: None) if last else (lambda: project_kv(hloc, wkv_ref, cos_ref, sin_ref, kn_ref, vn_ref))
-    reduce_gather(n_dev, me, part, x_ref, gain[...], x_out, h_out, hloc, d2d, stage, rem, sems, body)
-    if kind != "embed":
-        for i in range(1, n_dev):
-            send(i).wait_send()
-
-
-def boundary(n_dev, kind, index, ins, gain, kv_ins, rows_total):
+        copies[0].wait()
+        part[...] = jnp.dot(hid_ref[...], wd[...], preferred_element_type=F32)
+        copies[1].wait()
+        for cp in sends:
+            cp.wait_recv()
+        part[...] = jnp.dot(heads[...], wo[...], preferred_element_type=F32) + part[...]
+
+    def project_kv():
+        head_dim = kn_ref.shape[0]
+        half = head_dim // 2
+        starts[0].wait()
+        kv = lax.dot_general(wkv[...], hloc[...], (((1,), (1,)), ((), ())), preferred_element_type=F32)
+        k_lo, k_hi = kv[:half], kv[half:head_dim]
+        cos, sin = cosk_ref[...], sink_ref[...]
+        kn_ref[...] = jnp.concatenate([k_lo * cos - k_hi * sin, k_lo * sin + k_hi * cos], axis=0).astype(BF16).astype(F32)
+        vn_ref[...] = kv[head_dim:].astype(BF16).astype(F32)
+
+    reduce_gather(n_dev, me, part, x_ref, gain[...], x_out, h_out, hloc, d2d, stage, rem, sems, (lambda: None) if last else project_kv)
+    if not last:
+        h = h_out[...]
+        half = cos_ref.shape[0]
+        starts[1].wait()
+        qt = lax.dot_general(wq[...], h, (((1,), (1,)), ((), ())), preferred_element_type=F32)
+        cos, sin = cos_ref[...], sin_ref[...]
+        turned = []
+        for a in range(0, qt.shape[0], 2 * half):
+            lo, hi = qt[a:a + half], qt[a + half:a + 2 * half]
+            turned += [lo * cos - hi * sin, lo * sin + hi * cos]
+        q_buf[...] = jnp.concatenate(turned, axis=0).T.astype(BF16)
+        q_sends = exchange(q_buf, q_out, q_s, q_r)
+        for cp in q_sends:
+            cp.start()
+        q_out[block(me, rows)] = q_buf[block(me, rows)]
+        starts[2].wait()
+        starts[3].wait()
+        gate = jnp.dot(h, wg[...], preferred_element_type=F32)
+        up = jnp.dot(h, wu[...], preferred_element_type=F32)
+        hid_out[...] = (gate * jax.nn.sigmoid(gate) * up).astype(BF16)
+        for cp in q_sends:
+            cp.wait_recv()
+        for cp in q_sends:
+            cp.wait_send()
+    if not first:
+        for cp in sends:
+            cp.wait_send()
+
+
+def layer_step(n_dev, layer, ins, gain, proj, rows_total):
     vm = pl.BlockSpec(memory_space=pltpu.VMEM)
+    hbm = pl.BlockSpec(memory_space=pltpu.HBM)
+    first, last = len(ins) == 1, proj is None
     dim = gain.shape[1]
     rows = rows_total // n_dev
-    last = kv_ins is None
-    args = list(ins) + [gain] + ([] if last else list(kv_ins))
-    out_shape = [jax.ShapeDtypeStruct((rows, dim), BF16), jax.ShapeDtypeStruct((rows_total, dim), BF16)]
-    if not last:
-        head_dim = kv_ins[0].shape[0] // 2
-        out_shape += [jax.ShapeDtypeStruct((head_dim, rows), F32)] * 2
-    scratch = []
-    if kind != "embed":
-        width = ins[0].shape[1]
-        scratch = [pltpu.VMEM((rows_total, width), BF16), pltpu.VMEM((rows_total, dim), F32), pltpu.SemaphoreType.DMA((n_dev,)), pltpu.SemaphoreType.DMA((n_dev,))]
-    scratch += reduce_scratch(n_dev, rows, dim, BF16 if kind == "embed" else F32)
+    dma = pltpu.SemaphoreType.DMA
+    args = list(ins[:3]) + [gain] + list(ins[3:])
+    in_specs = [vm] * (2 if first else 4) + [hbm] * (0 if first else 2)
+    scratch = reduce_scratch(n_dev, rows, dim, BF16 if first else F32)
+    if not first:
+        width, hidden = ins[0].shape[1], ins[1].shape[1]
+        scratch += [pltpu.VMEM((rows_total, width), BF16), pltpu.VMEM((rows_total, dim), F32), pltpu.VMEM((width, dim), BF16), pltpu.VMEM((hidden, dim), BF16),
+                    dma((n_dev,)), dma((n_dev,)), dma((2,))]
+    if last:
+        out_shape = (jax.ShapeDtypeStruct((rows_total, dim), BF16),)
+    else:
+        cos_t, sin_t, cos_k, sin_k, wkv_t, wq_t, w_gate, w_up = proj
+        args += list(proj)
+        in_specs += [vm] * 4 + [hbm] * 4
+        width, hidden, kv = wq_t.shape[1], w_gate.shape[2], wkv_t.shape[1]
+        out_shape = (jax.ShapeDtypeStruct((rows, dim), BF16), jax.ShapeDtypeStruct((rows_total, width), BF16), jax.ShapeDtypeStruct((rows_total, hidden), BF16),
+                     jax.ShapeDtypeStruct((kv // 2, rows), F32), jax.ShapeDtypeStruct((kv // 2, rows), F32))
+        scratch += [pltpu.VMEM((rows_total, dim), BF16), pltpu.VMEM((rows_total, width), BF16), pltpu.VMEM((kv, dim), BF16), pltpu.VMEM((width, dim), BF16),
+                    pltpu.VMEM((dim, hidden), BF16), pltpu.VMEM((dim, hidden), BF16), dma((n_dev,)), dma((n_dev,)), dma((4,))]
     return pl.pallas_call(
-        functools.partial(boundary_kernel, n_dev, kind, last),
-        out_shape=tuple(out_shape),
-        in_specs=[vm] * len(args),
+        functools.partial(layer_kernel, n_dev, layer, first, last),
+        out_shape=out_shape,
+        in_specs=in_specs,
         out_specs=tuple([vm] * len(out_shape)),
         scratch_shapes=scratch,
-        compiler_params=pltpu.CompilerParams(vmem_limit_bytes=24 << 20, collective_id=index, has_side_effects=True),
-        cost_estimate=pl.CostEstimate(flops=20_000_000_000, bytes_accessed=8 << 20, transcendentals=0),
-        name=f"boundary{index}",
+        compiler_params=pltpu.CompilerParams(vmem_limit_bytes=40 << 20, collective_id=layer, has_side_effects=True),
+        cost_estimate=pl.CostEstimate(flops=20_000_000_000, bytes_accessed=16 << 20, transcendentals=0),
+        name=f"layer{layer}",
     )(*args)
-
-
-def project_kernel(n_dev, h_ref, wq_ref, cos_ref, sin_ref, wg_ref, wu_ref, wd_ref, q_out, mlp_ref, q_buf, hid, s_sem, r_sem):
-    me = lax.axis_index("tp")
-    bar = enter(n_dev, me)
-    rows = q_buf.shape[0] // n_dev
-    half = cos_ref.shape[0]
-    h = h_ref[...]
-    qt = lax.dot_general(wq_ref[...], h, (((1,), (1,)), ((), ())), preferred_element_type=F32)
-    cos, sin = cos_ref[...], sin_ref[...]
-    parts = []
-    for a in range(0, qt.shape[0], 2 * half):
-        lo, hi = qt[a:a + half], qt[a + half:a + 2 * half]
-        parts += [lo * cos - hi * sin, lo * sin + hi * cos]
-    q_buf[...] = jnp.concatenate(parts, axis=0).T.astype(BF16)
-    pl.semaphore_wait(bar, n_dev - 1)
-
-    def send(i):
-        d = lax.rem(me + i, n_dev)
-        return pltpu.make_async_remote_copy(q_buf.at[block(d, rows)], q_out.at[block(me, rows)], s_sem.at[i], r_sem.at[i], **device(d))
-
-    for i in range(1, n_dev):
-        send(i).start()
-    q_out[block(me, rows)] = q_buf[block(me, rows)]
-    gate = jnp.dot(h, wg_ref[...], preferred_element_type=F32)
-    up = jnp.dot(h, wu_ref[...], preferred_element_type=F32)
-    hid[...] = (gate * jax.nn.sigmoid(gate) * up).astype(BF16)
-    mlp_ref[...] = jnp.dot(hid[...], wd_ref[...], preferred_element_type=F32)
-    for i in range(1, n_dev):
-        send(i).wait_recv()
-    for i in range(1, n_dev):
-        send(i).wait_send()
-
-
-def project(n_dev, index, h, wq_t, cos_t, sin_t, wg, wu, wd):
-    vm = pl.BlockSpec(memory_space=pltpu.VMEM)
-    rows, dim = h.shape
-    width = wq_t.shape[0]
-    return pl.pallas_call(
-        functools.partial(project_kernel, n_dev),
-        out_shape=(jax.ShapeDtypeStruct((rows, width), BF16), jax.ShapeDtypeStruct((rows, dim), F32)),
-        in_specs=[vm] * 7,
-        out_specs=(vm, vm),
-        scratch_shapes=[pltpu.VMEM((rows, width), BF16), pltpu.VMEM((rows, wg.shape[1]), BF16), pltpu.SemaphoreType.DMA((n_dev,)), pltpu.SemaphoreType.DMA((n_dev,))],
-        compiler_params=pltpu.CompilerParams(vmem_limit_bytes=28 << 20, collective_id=index, has_side_effects=True),
-        cost_estimate=pl.CostEstimate(flops=6_000_000_000, bytes_accessed=14 << 20, transcendentals=0),
-        name=f"project{index}",
-    )(h, wq_t, cos_t, sin_t, wg, wu, wd)
 
 
 def solution(mesh):
@@ -376,26 +449,25 @@
         ang = inv_freq[:, None] * positions[None, :].astype(F32)
         cos_t = jnp.cos(ang)
         sin_t = jnp.sin(ang)
-        local_rows = steps * seqs
-        cos_k = lax.dynamic_slice_in_dim(cos_t, rank * local_rows, local_rows, axis=1)
-        sin_k = lax.dynamic_slice_in_dim(sin_t, rank * local_rows, local_rows, axis=1)
+        pos_k = (local_len[None, :] + jnp.arange(steps, dtype=jnp.int32)[:, None]).reshape(1, steps * seqs)
+        ang_k = inv_freq[:, None] * pos_k.astype(F32)
         wq_t = jnp.moveaxis(w_q, 1, 3).reshape(layers, width, dim)
         wkv_t = jnp.swapaxes(w_kv, 1, 2)
+        wo_r = w_o.reshape(layers, width, dim)
+        proj = (cos_t, sin_t, jnp.cos(ang_k), jnp.sin(ang_k), wkv_t, wq_t, w_gate, w_up)
         gains = [ln_scale[l][None] for l in range(layers)] + [final_scale[None]]
 
-        onehot = (tok[:, None] - rank * vocab_local == jnp.arange(vocab_local, dtype=jnp.int32)[None, :]).astype(BF16)
-        emb = jnp.dot(onehot, embedding, preferred_element_type=F32).astype(BF16)
-        x, h, k_new, v_new = boundary(n_dev, "embed", 0, (emb,), gains[0], (wkv_t[0], cos_k, sin_k), rows)
+        emb = lookup(tok - rank * vocab_local, embedding)
+        x, q_seq, hid, k_new, v_new = layer_step(n_dev, 0, (emb,), gains[0], proj, rows)
         outs = None
         for l in range(layers):
-            q_seq, mlp = project(n_dev, 1 + 2 * l, h, wq_t[l], cos_t, sin_t, w_gate[l], w_up[l], w_down[l])
             o, *outs = attention(l, steps, local_len, q_seq, k_new, v_new, kc, vc, outs)
-            kv_ins = (wkv_t[l + 1], cos_k, sin_k) if l + 1 < layers else None
-            x, h, *kv = boundary(n_dev, "layer", 2 + 2 * l, (o, w_o[l].reshape(width, dim), mlp, x), gains[l + 1], kv_ins, rows)
-            if kv:
-                k_new, v_new = kv
-        logits = lax.dot_general(h, embedding, (((1,), (1,)), ((), ())), preferred_element_type=F32) * dim ** -0.5
-        logits = logits.reshape(n_dev, steps, seqs, vocab_local).transpose(1, 0, 2, 3).reshape(steps, batch, vocab_local)
+            ins = (o, hid, x, wo_r, w_down)
+            if l + 1 < layers:
+                x, q_seq, hid, k_new, v_new = layer_step(n_dev, l + 1, ins, gains[l + 1], proj, rows)
+            else:
+                (h,) = layer_step(n_dev, l + 1, ins, gains[l + 1], None, rows)
+        logits = output_head(n_dev, steps, seqs, h, embedding)
         k_out, v_out = outs
         return logits, jnp.swapaxes(k_out, 2, 3), jnp.swapaxes(v_out, 2, 3)
 

time: 182 us -> 179 us (0.984)
  matrix products: 19.1 us -> 0 us
  Pallas kernels: 134 us -> 150 us
    dot_general x2 -> x0, matrix products: 19.1 us -> none  [the longest x1 10.2 us: device_fn(): lax.dot_general(h, embedding, (((1,), (1,)), ((), ())), preferred_element...]
    pallas_call x5, Pallas kernels: 119 us -> 135 us  [the longest x3 117 us: layer_step(): pl.pallas_call(functools.partial(layer_kernel, n_dev, layer, first, last)...]
    unnamed x54 -> x34, local copies, waits for them, and re-layouts: 9.56 us -> 24.2 us
    squeeze x3 -> x0, local copies, waits for them, and re-layouts: 10.8 us -> none  [the longest x1 5.13 us: device_fn(): w_down[l]]
    transpose x1 -> x0, local copies, waits for them, and re-layouts: 3.84 us -> none  [device_fn(): logits.reshape(n_dev, steps, seqs, vocab_local).transpose(1, 0, 2, 3)]
where the time goes in v3:
time: 179 us; the launch traced here: 178 us
  Pallas kernels  150 us (84%)
  local copies, waits for them, and re-layouts  26.1 us (15%)
    pallas_call x3, Pallas kernels, layer_step(): pl.pallas_call(functools.partial(layer_kernel, n_dev, layer, first, last)...  117 us
    unnamed x34, local copies, waits for them, and re-layouts  24.2 us
    pallas_call x2, Pallas kernels, attention(): pl.pallas_call(functools.partial(attn_kernel, layer, outs is not None, st...  15.2 us
    pallas_call x1, Pallas kernels, lookup(): pl.pallas_call(lookup_kernel, out_shape=jax.ShapeDtypeStruct((rows, dim),...  10.4 us
    pallas_call x1, Pallas kernels, output_head(): pl.pallas_call(functools.partial(logits_kernel, n_dev, seqs, dim ** (-0.5...  7.01 us

profile of v3, /device:TPU:0, one launch (start us, length us, event | category | flops | bytes accessed | tf_op | source)
XLA Modules:
  0.0 178.0 jit_solution(8550945935422991072)
XLA Ops:
  0.6 0.7 dynamic_slice.3.len_ref
  1.4 0.1 convert_element_type.25
  1.5 0.2 multiply_sine_fusion.1
  1.6 0.7 add.44
  2.4 0.1 convert_element_type.23
  2.5 0.2 multiply_sine_fusion
  2.7 0.7 broadcast_subtract_fusion
  3.4 0.1 sub.14
  3.5 0.1 sub.16.tok_ref
  3.6 0.0 copy-start
  3.6 5.7 %copy-done = bf16[3200,2560]{1,0:T(8,128)(2,1)S(1)} copy-done((bf16[3200,2560]{1,0:T(8,128)(2,1)S(1)}, bf16[3200,2560]{1,0:T(8,128)(2,1)}, u32[]{:S(2)}) %copy-start) | copy-done | bytes 16384024
  9.3 0.0 copy-start.11
  9.3 0.0 slice-start
  9.3 0.0 slice-start.2
  9.3 10.4 %lookup.1.refs_0_ = bf16[256,2560]{1,0:T(8,128)(2,1)S(1)} custom-call(s32[256]{0:T(256)S(1)} %sub.16.tok_ref, bf16[3200,2560]{1,0:T(8,128)(2,1)S(1)} %copy-done), custom_call_target="tpu_custom_call" | custom-call | flops 1000000000 | bytes 2097152 | tf_op jit(solution)/shard_map/lookup/pallas_call | solution.py:264
  19.7 0.0 copy-done.11
  19.7 0.0 copy-start.2
  19.7 2.9 %copy-done.2 = bf16[2,2560,640]{2,1,0:T(8,128)(2,1)S(1)} copy-done((bf16[2,2560,640]{2,1,0:T(8,128)(2,1)S(1)}, bf16[2,2560,640]{2,1,0:T(8,128)(2,1)}, u32[]{:S(2)}) %copy-start.2) | copy-done | bytes 6553624
  22.6 0.0 copy-start.5
  22.6 1.4 copy-done.5
  24.0 0.0 copy-start.7
  24.0 1.4 copy-done.7
  25.4 0.0 slice-start.1
  25.4 0.0 slice-start.3
  25.4 33.4 %layer0.1 = (bf16[16,2560]{1,0:T(8,128)(2,1)S(1)}, bf16[256,160]{1,0:T(8,128)(2,1)S(1)}, bf16[256,640]{1,0:T(8,128)(2,1)S(1)}, f32[80,16]{1,0:T(8,128)S(1)}, f32[80,16]{1,0:T(8,128)S(1)}) custom-call(bf16[256,2560]{1,0:T(8,128)(2,1)S(1)} %lookup.1.refs_0_, f32[1,2560]{1,0:T(1,128)S(1)} %get-tuple-element.36.refs_1_, ...), custom_call_target="tpu_custom_call" | custom-call | flops 20000000000 | bytes 16777216 | tf_op jit(solution)/shard_map/layer0/pallas_call | solution.py:415
  58.8 0.0 slice-done
  58.8 0.0 slice-done.2
  58.8 0.0 slice-done.1
  58.8 0.0 slice-done.3
  58.9 0.0 copy-start.8
  58.9 0.0 copy-start.9
  58.9 7.5 %attend0.1 = (bf16[256,160]{1,0:T(8,128)(2,1)S(1)}, bf16[2,8,80,2048]{3,2,1,0:T(8,128)(2,1)}, bf16[2,8,80,2048]{3,2,1,0:T(8,128)(2,1)}) custom-call(s32[8]{0:T(128)S(1)} %dynamic_slice.3.len_ref, bf16[256,160]{1,0:T(8,128)(2,1)S(1)} %get-tuple-element.19.q_ref, f32[80,16]{1,0:T(8,128)S(1)} %get-tuple-element.20.kn_ref, ...), custom_call_target="tpu_custom_call" | custom-call | flops 2000000000 | bytes 22020096 | tf_op jit(solution)/shard_map/attend0/pallas_call | solution.py:112
  66.4 0.0 copy-done.8
  66.4 0.0 copy-done.9
  66.4 0.0 copy-start.3
  66.4 2.9 %copy-done.3 = bf16[2,640,2560]{2,1,0:T(8,128)(2,1)S(1)} copy-done((bf16[2,640,2560]{2,1,0:T(8,128)(2,1)S(1)}, bf16[2,640,2560]{2,1,0:T(8,128)(2,1)}, u32[]{:S(2)}) %copy-start.3) | copy-done | bytes 6553624
  69.3 0.0 copy-start.6
  69.3 1.4 copy-done.6
  70.7 44.9 %layer1.1 = (bf16[16,2560]{1,0:T(8,128)(2,1)S(1)}, bf16[256,160]{1,0:T(8,128)(2,1)S(1)}, bf16[256,640]{1,0:T(8,128)(2,1)S(1)}, f32[80,16]{1,0:T(8,128)S(1)}, f32[80,16]{1,0:T(8,128)S(1)}) custom-call(bf16[256,160]{1,0:T(8,128)(2,1)S(1)} %get-tuple-element.22.refs_0_, bf16[256,640]{1,0:T(8,128)(2,1)S(1)} %get-tuple-element.23.refs_1_, ...), custom_call_target="tpu_custom_call" | custom-call | flops 20000000000 | bytes 16777216 | tf_op jit(solution)/shard_map/layer1/pallas_call | solution.py:415
  115.6 0.0 copy-start.12
  115.7 0.0 copy-start.10
  115.7 7.7 %attend1.1 = (bf16[256,160]{1,0:T(8,128)(2,1)S(1)}, bf16[2,8,80,2048]{3,2,1,0:T(8,128)(2,1)}, bf16[2,8,80,2048]{3,2,1,0:T(8,128)(2,1)}) custom-call(s32[8]{0:T(128)S(1)} %dynamic_slice.3.len_ref, bf16[256,160]{1,0:T(8,128)(2,1)S(1)} %get-tuple-element.25.q_ref, f32[80,16]{1,0:T(8,128)S(1)} %get-tuple-element.26.kn_ref, ...), custom_call_target="tpu_custom_call", output_to_operand_aliasing={{1}: (6, {}), {2}: (7, {})} | custom-call | flops 2000000000 | bytes 22020096 | tf_op jit(solution)/shard_map/attend1/pallas_call | solution.py:112
  123.4 0.0 copy-done.12
  123.4 0.0 copy-done.10
  123.4 0.0 copy-start.4
  123.4 2.9 %copy-done.4 = bf16[2,640,2560]{2,1,0:T(8,128)(2,1)S(1)} copy-done((bf16[2,640,2560]{2,1,0:T(8,128)(2,1)S(1)}, bf16[2,640,2560]{2,1,0:T(8,128)(2,1)}, u32[]{:S(2)}) %copy-start.4) | copy-done | bytes 6553624
  126.3 39.0 %layer2.1.h_ref = bf16[256,2560]{1,0:T(8,128)(2,1)S(1)} custom-call(bf16[256,160]{1,0:T(8,128)(2,1)S(1)} %get-tuple-element.30.refs_0_, bf16[256,640]{1,0:T(8,128)(2,1)S(1)} %get-tuple-element.31.refs_1_, bf16[16,2560]{1,0:T(8,128)(2,1)S(1)} %get-tuple-element.32.refs_2_, f32[1,2560]{1,0:T(1,128)S(1)} %broadcast_in_dim.2.refs_3_, ...), custom_call_target="tpu_custom_call" | custom-call | flops 20000000000 | bytes 16777216 | tf_op jit(solution)/shard_map/layer2/pallas_call | solution.py:415
  165.3 0.0 copy-start.1
  165.3 5.6 %copy-done.1 = bf16[3200,2560]{1,0:T(8,128)(2,1)S(1)} copy-done((bf16[3200,2560]{1,0:T(8,128)(2,1)S(1)}, bf16[3200,2560]{1,0:T(8,128)(2,1)}, u32[]{:S(2)}) %copy-start.1) | copy-done | bytes 16384024
  171.0 7.0 %head.1 = f32[2,128,3200]{2,1,0:T(8,128)} custom-call(bf16[256,2560]{1,0:T(8,128)(2,1)S(1)} %layer2.1.h_ref, bf16[3200,2560]{1,0:T(8,128)(2,1)S(1)} %copy-done.1), custom_call_target="tpu_custom_call" | custom-call | flops 4000000000 | bytes 20971520 | tf_op jit(solution)/shard_map/head/pallas_call | solution.py:289
  (8 shorter events, 0.1 us)
Async XLA Ops:
  3.6 5.7 %copy-start = (bf16[3200,2560]{1,0:T(8,128)(2,1)S(1)}, bf16[3200,2560]{1,0:T(8,128)(2,1)}, u32[]{:S(2)}) copy-start(bf16[3200,2560]{1,0:T(8,128)(2,1)} %e_ref.1) | copy-start | bytes 49152004
  9.3 10.4 %copy-start.11 = (f32[2,2560]{1,0:T(2,128)S(1)}, f32[2,2560]{1,0:T(2,128)}, u32[]{:S(2)}) copy-start(f32[2,2560]{1,0:T(2,128)} %param.16) | copy-start | bytes 61444
  9.3 49.5 %slice-start = ((s8[5242880]{0:T(1024)(128)(4,1)}), s8[4194304]{0:T(1024)(128)(4,1)S(1)}, s32[]{:S(2)}) async-start(s8[5242880]{0:T(1024)(128)(4,1)} %bitcast.10), calls=%async_computation | async-start | bytes 8388608
  9.3 49.5 %slice-start.2 = ((s8[5242880]{0:T(1024)(128)(4,1)}), s8[4194304]{0:T(1024)(128)(4,1)S(1)}, s32[]{:S(2)}) async-start(s8[5242880]{0:T(1024)(128)(4,1)} %bitcast.14), calls=%async_computation.2 | async-start | bytes 8388608
  19.7 2.9 %copy-start.2 = (bf16[2,2560,640]{2,1,0:T(8,128)(2,1)S(1)}, bf16[2,2560,640]{2,1,0:T(8,128)(2,1)}, u32[]{:S(2)}) copy-start(bf16[2,2560,640]{2,1,0:T(8,128)(2,1)} %refs_12_.1) | copy-start | bytes 19660804
  22.6 1.4 copy-start.5
  24.0 1.4 copy-start.7
  25.4 33.4 %slice-start.1 = ((s8[5242880]{0:T(1024)(128)(4,1)}), s8[1048576]{0:T(1024)(128)(4,1)S(1)}, s32[]{:S(2)}) async-start(s8[5242880]{0:T(1024)(128)(4,1)} %bitcast.10), calls=%async_computation.1 | async-start | bytes 2097152
  25.4 33.4 %slice-start.3 = ((s8[5242880]{0:T(1024)(128)(4,1)}), s8[1048576]{0:T(1024)(128)(4,1)S(1)}, s32[]{:S(2)}) async-start(s8[5242880]{0:T(1024)(128)(4,1)} %bitcast.14), calls=%async_computation.3 | async-start | bytes 2097152
  58.9 7.5 %copy-start.8 = (bf16[2,2560,2,80]{1,3,2,0:T(8,128)(2,1)S(1)}, bf16[2,2560,2,80]{1,3,2,0:T(8,128)(2,1)}, u32[]{:S(2)}) copy-start(bf16[2,2560,2,80]{1,3,2,0:T(8,128)(2,1)} %param.17) | copy-start | bytes 4915204
  58.9 7.5 %copy-start.9 = (bf16[2,2,80,2560]{3,2,1,0:T(8,128)(2,1)S(1)}, bf16[2,2,80,2560]{3,2,1,0:T(8,128)(2,1)}, u32[]{:S(2)}) copy-start(bf16[2,2,80,2560]{3,2,1,0:T(8,128)(2,1)} %param.19) | copy-start | bytes 4915204
  66.4 2.9 %copy-start.3 = (bf16[2,640,2560]{2,1,0:T(8,128)(2,1)S(1)}, bf16[2,640,2560]{2,1,0:T(8,128)(2,1)}, u32[]{:S(2)}) copy-start(bf16[2,640,2560]{2,1,0:T(8,128)(2,1)} %refs_5_.3) | copy-start | bytes 19660804
  69.3 1.4 copy-start.6
  115.6 7.7 %copy-start.12 = (f32[2560]{0:T(1024)S(1)}, f32[2560]{0:T(1024)}, u32[]{:S(2)}) copy-start(f32[2560]{0:T(1024)} %param.23) | copy-start | bytes 30724
  115.7 7.7 %copy-start.10 = (bf16[2,2,80,2560]{3,2,1,0:T(8,128)(2,1)S(1)}, bf16[2,2,80,2560]{3,2,1,0:T(8,128)(2,1)}, u32[]{:S(2)}) copy-start(bf16[2,2,80,2560]{3,2,1,0:T(8,128)(2,1)} %param.19) | copy-start | bytes 4915204
  123.4 2.9 %copy-start.4 = (bf16[2,640,2560]{2,1,0:T(8,128)(2,1)S(1)}, bf16[2,640,2560]{2,1,0:T(8,128)(2,1)}, u32[]{:S(2)}) copy-start(bf16[2,640,2560]{2,1,0:T(8,128)(2,1)} %refs_5_.3) | copy-start | bytes 19660804
  165.3 5.7 %copy-start.1 = (bf16[3200,2560]{1,0:T(8,128)(2,1)S(1)}, bf16[3200,2560]{1,0:T(8,128)(2,1)}, u32[]{:S(2)}) copy-start(bf16[3200,2560]{1,0:T(8,128)(2,1)} %e_ref.1) | copy-start | bytes 49152004

commit v4 on v3

--- a/solution.py
+++ b/solution.py
@@ -10,12 +10,13 @@
 LN_EPS = 1e-6
 F32 = jnp.float32
 BF16 = jnp.bfloat16
+BIG_VMEM = 62 * 1024 * 1024 + 512 * 1024
 
 
 def attn_kernel(layer, has_alias, steps, seqs, len_ref, q_ref, kn_ref, vn_ref, kc_ref, vc_ref, *rest):
     if has_alias:
         rest = rest[2:]
-    o_ref, ko_ref, vo_ref, kbuf, vbuf, qa, qb, oa, ob, isem, osem = rest
+    o_ref, ko_ref, vo_ref, kbuf, vbuf, wide, qa, qb, oa, ob, isem, osem = rest
     head_dim, seq_len = kbuf.shape[1], kbuf.shape[2]
     rows_per = steps * seqs
     srcs = q_ref.shape[0] // rows_per
@@ -36,17 +37,21 @@
     qb[...] = jnp.zeros_like(qb)
     qb[:, :width2 - 128] = q_ref[:, 128:].astype(F32)
     lane = lax.broadcasted_iota(jnp.int32, (head_dim, 128), 1)
-    for s in range(seqs):
+    for c in range(rows_per):
+        for i, new in enumerate((kn_ref, vn_ref)):
+            wide[i, c] = jnp.broadcast_to(new[:, c:c + 1], (head_dim, 128))
+    first = lax.axis_index("tp") * seqs
+
+    def update(s):
         for cp in in_copies(s):
             cp.wait()
         for t in range(steps):
-            p = len_ref[s] + t
+            p = len_ref[first + s] + t
             base = pl.multiple_of((p // 128) * 128, 128)
             hit = lane == (p - base)
-            c = t * seqs + s
-            for buf, new in ((kbuf, kn_ref), (vbuf, vn_ref)):
+            for i, buf in enumerate((kbuf, vbuf)):
                 tile = buf[s, :, pl.ds(base, 128)].astype(F32)
-                buf[s, :, pl.ds(base, 128)] = jnp.where(hit, new[:, c:c + 1], tile).astype(BF16)
+                buf[s, :, pl.ds(base, 128)] = jnp.where(hit, wide[i, t * seqs + s], tile).astype(BF16)
         for cp in out_copies(s):
             cp.start()
 
@@ -55,7 +60,7 @@
     scale = head_dim ** -0.5
 
     def attend(s, width):
-        p = len_ref[s]
+        p = len_ref[first + s]
         at = [pl.ds(t * seqs + s, srcs, stride=rows_per) for t in range(steps)]
         qcat = jnp.concatenate([jnp.concatenate([qa[i, :], qb[i, :]], axis=1)[:, :width2] for i in at], axis=0)
         q2 = jnp.concatenate([jnp.where(half, qcat, 0.0), jnp.where(half, 0.0, qcat)], axis=0).astype(BF16)
@@ -82,7 +87,8 @@
 
     @pl.loop(0, seqs)
     def _(s):
-        last = len_ref[s] + (steps - 1)
+        update(s)
+        last = len_ref[first + s] + (steps - 1)
         lo = 0
         for w in widths:
             @pl.when((last >= lo) & (last < w))
@@ -97,12 +103,12 @@
             cp.wait()
 
 
-def attention(layer, steps, local_len, q, k_new, v_new, kc, vc, outs):
+def attention(layer, steps, lengths, q, k_new, v_new, kc, vc, outs):
     layers, seqs, head_dim, seq_len = kc.shape
     rows, width = q.shape
     any_spec = pl.BlockSpec(memory_space=pltpu.HBM)
     vm = pl.BlockSpec(memory_space=pltpu.VMEM)
-    args = [local_len, q, k_new, v_new, kc, vc]
+    args = [lengths, q, k_new, v_new, kc, vc]
     in_specs = [pl.BlockSpec(memory_space=pltpu.SMEM), vm, vm, vm, any_spec, any_spec]
     aliases = {}
     if outs is not None:
@@ -117,6 +123,7 @@
         scratch_shapes=[
             pltpu.VMEM((seqs, head_dim, seq_len), BF16),
             pltpu.VMEM((seqs, head_dim, seq_len), BF16),
+            pltpu.VMEM((2, steps * seqs, head_dim, 128), F32),
             pltpu.VMEM((rows, 128), F32),
             pltpu.VMEM((rows, 128), F32),
             pltpu.VMEM((rows, 128), F32),
@@ -125,7 +132,7 @@
             pltpu.SemaphoreType.DMA((2, seqs)),
         ],
         input_output_aliases=aliases,
-        compiler_params=pltpu.CompilerParams(vmem_limit_bytes=24 << 20),
+        compiler_params=pltpu.CompilerParams(vmem_limit_bytes=BIG_VMEM),
         cost_estimate=pl.CostEstimate(flops=2_000_000_000, bytes_accessed=21 << 20, transcendentals=1 << 20),
         name=f"attend{layer}",
     )(*args)
@@ -160,122 +167,192 @@
     return (centred * lax.rsqrt(row_var + LN_EPS) * gain).astype(BF16)
 
 
-def reduce_gather(n_dev, me, part, x_ref, gain, x_out, h_out, hloc, d2d, stage, rem, sems, while_gathering):
-    d2d_s, d2d_r, far_s, far_r, ag_s, ag_r, fw_s, fw_r = sems
+def column_groups(dim):
+    tiles = dim // 128
+    cuts = [0] + [128 * ((tiles * (i + 1) + 2) // 3) for i in range(3)]
+    return [pl.ds(lo, hi - lo) for lo, hi in zip(cuts[:-1], cuts[1:])]
+
+
+def reduce_gather(n_dev, me, part, x_ref, gain, x_out, h_out, hloc, d2d, acc, r1, r2, r3, sems, while_gathering):
+    d2d_s, d2d_r, s1, q1, s2, q2, s3, q3, ag_s, ag_r, fw_s, fw_r = sems
     n_chips = n_dev // 2
-    n_bits = n_chips.bit_length() - 1
     rows = hloc.shape[0]
     chip, core = me // 2, lax.rem(me, 2)
     sibling = chip * 2 + 1 - core
-    order = sorted(range(n_chips), key=lambda j: -bin(j).count("1"))
+    cols = column_groups(hloc.shape[1])
+    orders = [(1, 2, 4), (2, 4, 1), (4, 1, 2)]
+    by_distance = sorted(range(n_chips), key=lambda j: -bin(j).count("1"))
+    where = {j: chip_at(chip, j, 3) for j in range(n_chips)}
+    peer = {a: device(where[a] * 2 + core) for a in (1, 2, 4)}
+    copy = pltpu.make_async_remote_copy
 
     def pre(j):
-        c = chip_at(chip, j, n_bits)
-        return pltpu.make_async_remote_copy(part.at[block(c * 2 + 1 - core, rows)], d2d.at[j], d2d_s.at[j], d2d_r.at[j], **device(sibling))
-
-    def far(j):
-        c = chip_at(chip, j, n_bits)
-        return pltpu.make_async_remote_copy(stage.at[j], rem.at[j], far_s.at[j], far_r.at[j], **device(c * 2 + core))
-
-    for j in order:
+        return copy(part.at[block(where[j] * 2 + 1 - core, rows)], d2d.at[j], d2d_s.at[j], d2d_r.at[j], **device(sibling))
+
+    def halve1(g, i):
+        a, b, c = orders[g]
+        j = (b + c, b, c, 0)[i]
+        return j, copy(acc.at[j + a, :, cols[g]], r1.at[i, :, cols[g]], s1.at[g, i], q1.at[g, i], **peer[a])
+
+    def halve2(g, i):
+        a, b, c = orders[g]
+        j = (c, 0)[i]
+        return j, copy(acc.at[j + b, :, cols[g]], r2.at[i, :, cols[g]], s2.at[g, i], q2.at[g, i], **peer[b])
+
+    def halve3(g):
+        c = orders[g][2]
+        return copy(acc.at[c, :, cols[g]], r3.at[:, cols[g]], s3.at[g], q3.at[g], **peer[c])
+
+    def add(j, g, other):
+        acc[j, :, cols[g]] = (acc[j, :, cols[g]].astype(F32) + other.astype(F32)).astype(acc.dtype)
+
+    for j in by_distance:
         pre(j).start()
-    for j in order[:-1]:
+    for j in by_distance:
         pre(j).wait_recv()
-        c = chip_at(chip, j, n_bits)
-        stage[j] = (part[block(c * 2 + core, rows)].astype(F32) + d2d[j].astype(F32)).astype(stage.dtype)
-        far(j).start()
-    pre(0).wait_recv()
-    acc = part[block(me, rows)].astype(F32) + d2d[0].astype(F32)
-    for j in reversed(order[:-1]):
-        far(j).wait_recv()
-        acc = acc + rem[j].astype(F32)
+        acc[j] = (part[block(where[j] * 2 + core, rows)].astype(F32) + d2d[j].astype(F32)).astype(acc.dtype)
+        for g in range(3):
+            for i in range(4):
+                k, cp = halve1(g, i)
+                if k + orders[g][0] == j:
+                    cp.start()
+    for i in range(4):
+        for g in range(3):
+            j, cp = halve1(g, i)
+            cp.wait_recv()
+            add(j, g, r1[i, :, cols[g]])
+            if i < 2:
+                halve2(g, i)[1].start()
+    for g in range(3):
+        j, cp = halve2(g, 0)
+        cp.wait_recv()
+        add(j, g, r2[0, :, cols[g]])
+        halve3(g).start()
+    for g in range(3):
+        halve2(g, 1)[1].wait_recv()
+        add(0, g, r2[1, :, cols[g]])
+    for g in range(3):
+        halve3(g).wait_recv()
+    total = acc[0].astype(F32) + r3[...].astype(F32)
     if x_ref is not None:
-        acc = x_ref[...].astype(F32) + acc
-    x_new = acc.astype(BF16)
+        total = x_ref[...].astype(F32) + total
+    x_new = total.astype(BF16)
     if x_out is not None:
         x_out[...] = x_new
     hloc[...] = norm_rows(x_new.astype(F32), gain)
     h_out[block(me, rows)] = hloc[...]
 
-    def gather(j):
-        c = chip_at(chip, j, n_bits)
-        return pltpu.make_async_remote_copy(hloc, h_out.at[block(me, rows)], ag_s.at[j], ag_r.at[j], **device(c * 2 + core if j else sibling))
-
-    def relay(j):
-        c = chip_at(chip, j, n_bits)
-        blk = h_out.at[block(c * 2 + core, rows)]
-        return pltpu.make_async_remote_copy(blk, blk, fw_s.at[j], fw_r.at[j], **device(sibling))
-
-    for j in order:
-        gather(j).start()
+    def spread(g, j, axis):
+        mine = block(where[j] * 2 + core, rows)
+        src = hloc.at[:, cols[g]] if j == 0 else h_out.at[mine, cols[g]]
+        return copy(src, h_out.at[mine, cols[g]], ag_s.at[g, j + axis], ag_r.at[g, j + axis], **peer[axis])
+
+    def arrive(g, j):
+        a, b, c = orders[g]
+        last = c if j & c else b if j & b else a
+        cp = spread(g, j - last, last)
+        cp.wait_recv()
+        after = {a: (b, c), b: (c,), c: ()}[last]
+        for axis in after:
+            spread(g, j, axis).start()
+        relay(g, j).start()
+        return cp
+
+    def relay(g, j):
+        blk = h_out.at[block(where[j] * 2 + core, rows), cols[g]]
+        return copy(blk, blk, fw_s.at[g, j], fw_r.at[g, j], **device(sibling))
+
+    for i in range(3):
+        for g in range(3):
+            spread(g, 0, orders[g][i]).start()
+    own = copy(hloc, h_out.at[block(me, rows)], fw_s.at[0, 0], fw_r.at[0, 0], **device(sibling))
+    own.start()
     while_gathering()
-    for j in reversed(order[:-1]):
-        gather(j).wait_recv()
-        relay(j).start()
-    gather(0).wait_recv()
-    for j in order[:-1]:
-        relay(j).wait_recv()
-    for j in order:
+    for pick in ((0,), (1,), (0, 1), (2,), (0, 2), (1, 2), (0, 1, 2)):
+        for g in range(3):
+            arrive(g, sum(orders[g][i] for i in pick))
+    own.wait_recv()
+    for j in range(1, n_chips):
+        for g in range(3):
+            relay(g, j).wait_recv()
+    for j in range(n_chips):
         pre(j).wait_send()
-        gather(j).wait_send()
-        if j:
-            far(j).wait_send()
-            relay(j).wait_send()
+    own.wait_send()
+    for g in range(3):
+        for i in range(4):
+            halve1(g, i)[1].wait_send()
+        for i in range(2):
+            halve2(g, i)[1].wait_send()
+        halve3(g).wait_send()
+        for j in range(1, n_chips):
+            a, b, c = orders[g]
+            last = c if j & c else b if j & b else a
+            spread(g, j - last, last).wait_send()
+            relay(g, j).wait_send()
 
 
 def reduce_scratch(n_dev, rows, dim, dtype):
     n_chips = n_dev // 2
-    return [pltpu.VMEM((rows, dim), BF16)] + [pltpu.VMEM((n_chips, rows, dim), dtype)] * 3 + [pltpu.SemaphoreType.DMA((n_chips,))] * 8
-
-
-def lookup_kernel(tok_ref, emb_ref, out_ref, buf, row32, out32, sem):
+    dma = pltpu.SemaphoreType.DMA
+    return ([pltpu.VMEM((rows, dim), BF16)] + [pltpu.VMEM((n_chips, rows, dim), dtype)] * 2
+            + [pltpu.VMEM((4, rows, dim), dtype), pltpu.VMEM((2, rows, dim), dtype), pltpu.VMEM((rows, dim), dtype)]
+            + [dma((n_chips,))] * 2 + [dma((3, 4))] * 2 + [dma((3, 2))] * 2 + [dma((3,))] * 2 + [dma((3, n_chips))] * 4)
+
+
+def lookup_kernel(n_dev, tok_ref, emb_ref, out_ref, found, buf, row32, out32, sem):
     n_rows, group = buf.shape[0], buf.shape[1]
     vocab = emb_ref.shape[0]
-
-    def fetch(i):
-        first = pl.multiple_of((tok_ref[i] // group) * group, group)
-        return pltpu.make_async_copy(emb_ref.at[pl.ds(first, group), :], buf.at[i], sem.at[i])
-
-    def each(fn):
-        @pl.loop(0, n_rows // 8)
-        def _(base):
-            for u in range(8):
-                i = base * 8 + u
-                tok = tok_ref[i]
-
-                @pl.when((tok >= 0) & (tok < vocab))
-                def _():
-                    fn(i, tok)
-
-    each(lambda i, tok: fetch(i).start())
+    steps, batch = tok_ref.shape
+    seqs = batch // n_dev
+    first = lax.axis_index("tp") * vocab
+
+    def scan(d, count):
+        for t in range(steps):
+            for s in range(seqs):
+                tok = tok_ref[t, d * seqs + s] - first
+                found[0, count] = (d * steps + t) * seqs + s
+                found[1, count] = tok
+                count = count + ((tok >= 0) & (tok < vocab)).astype(jnp.int32)
+        return count
+
+    count = lax.fori_loop(0, n_dev, scan, jnp.int32(0))
+
+    def fetch(n):
+        at = pl.multiple_of((found[1, n] // group) * group, group)
+        return pltpu.make_async_copy(emb_ref.at[pl.ds(at, group), :], buf.at[n], sem.at[n])
+
+    @pl.loop(0, count)
+    def _(n):
+        fetch(n).start()
+
     out32[...] = jnp.zeros_like(out32)
 
-    def place(i, tok):
-        fetch(i).wait()
-        row32[...] = buf[i].astype(F32)
-        out32[pl.ds(i, 1), :] = row32[pl.ds(lax.rem(tok, group), 1), :]
-
-    each(place)
+    @pl.loop(0, count)
+    def _(n):
+        fetch(n).wait()
+        row32[...] = buf[n].astype(F32)
+        out32[pl.ds(found[0, n], 1), :] = row32[pl.ds(lax.rem(found[1, n], group), 1), :]
+
     out_ref[...] = out32[...].astype(BF16)
 
 
-def lookup(tok, embedding):
-    rows, dim, group = tok.shape[0], embedding.shape[1], 16
+def lookup(n_dev, tokens, embedding):
+    rows, dim, group = tokens.size, embedding.shape[1], 16
     return pl.pallas_call(
-        lookup_kernel,
+        functools.partial(lookup_kernel, n_dev),
         out_shape=jax.ShapeDtypeStruct((rows, dim), BF16),
         in_specs=[pl.BlockSpec(memory_space=pltpu.SMEM), pl.BlockSpec(memory_space=pltpu.HBM)],
         out_specs=pl.BlockSpec(memory_space=pltpu.VMEM),
-        scratch_shapes=[pltpu.VMEM((rows, group, dim), BF16), pltpu.VMEM((group, dim), F32), pltpu.VMEM((rows, dim), F32), pltpu.SemaphoreType.DMA((rows,))],
-        compiler_params=pltpu.CompilerParams(vmem_limit_bytes=32 << 20),
+        scratch_shapes=[pltpu.SMEM((2, rows), jnp.int32), pltpu.VMEM((rows, group, dim), BF16), pltpu.VMEM((group, dim), F32), pltpu.VMEM((rows, dim), F32), pltpu.SemaphoreType.DMA((rows,))],
+        compiler_params=pltpu.CompilerParams(vmem_limit_bytes=BIG_VMEM),
         cost_estimate=pl.CostEstimate(flops=1_000_000_000, bytes_accessed=2 << 20, transcendentals=0),
         name="lookup",
-    )(tok, embedding)
+    )(tokens, embedding)
 
 
 def logits_kernel(n_dev, seqs, scale, h_ref, e_ref, out_ref):
     steps = out_ref.shape[0]
-    acc = lax.dot_general(h_ref[...], e_ref[...], (((1,), (1,)), ((), ())), preferred_element_type=F32) * scale
+    acc = (lax.dot_general(e_ref[...], h_ref[...], (((1,), (1,)), ((), ())), preferred_element_type=F32) * scale).T
     for d in range(n_dev):
         for t in range(steps):
             at = (d * steps + t) * seqs
@@ -292,7 +369,7 @@
         out_shape=jax.ShapeDtypeStruct((steps, rows // steps, vocab), F32),
         in_specs=[pl.BlockSpec((rows, dim), lambda i: (0, 0)), pl.BlockSpec((tile, dim), lambda i: (i, 0))],
         out_specs=pl.BlockSpec((steps, rows // steps, tile), lambda i: (0, 0, i)),
-        compiler_params=pltpu.CompilerParams(vmem_limit_bytes=28 << 20),
+        compiler_params=pltpu.CompilerParams(vmem_limit_bytes=BIG_VMEM),
         cost_estimate=pl.CostEstimate(flops=4_000_000_000, bytes_accessed=20 << 20, transcendentals=0),
         name="head",
     )(h, embedding)
@@ -311,7 +388,7 @@
         x_out, q_out, hid_out, kn_ref, vn_ref = take(5)
     else:
         (h_out,) = take(1)
-    hloc, d2d, stage, rem, *sems = take(12)
+    hloc, d2d, acc, r1, r2, r3, *sems = take(18)
     copies = []
     if not first:
         heads, part, wo, wd, a2a_s, a2a_r, w_sem = take(7)
@@ -357,7 +434,7 @@
         kn_ref[...] = jnp.concatenate([k_lo * cos - k_hi * sin, k_lo * sin + k_hi * cos], axis=0).astype(BF16).astype(F32)
         vn_ref[...] = kv[head_dim:].astype(BF16).astype(F32)
 
-    reduce_gather(n_dev, me, part, x_ref, gain[...], x_out, h_out, hloc, d2d, stage, rem, sems, (lambda: None) if last else project_kv)
+    reduce_gather(n_dev, me, part, x_ref, gain[...], x_out, h_out, hloc, d2d, acc, r1, r2, r3, sems, (lambda: None) if last else project_kv)
     if not last:
         h = h_out[...]
         half = cos_ref.shape[0]
@@ -418,7 +495,7 @@
         in_specs=in_specs,
         out_specs=tuple([vm] * len(out_shape)),
         scratch_shapes=scratch,
-        compiler_params=pltpu.CompilerParams(vmem_limit_bytes=40 << 20, collective_id=layer, has_side_effects=True),
+        compiler_params=pltpu.CompilerParams(vmem_limit_bytes=BIG_VMEM, collective_id=layer, has_side_effects=True),
         cost_estimate=pl.CostEstimate(flops=20_000_000_000, bytes_accessed=16 << 20, transcendentals=0),
         name=f"layer{layer}",
     )(*args)
@@ -443,7 +520,6 @@
         def by_device(per_step):
             return per_step.reshape(steps, n_dev, seqs).transpose(1, 0, 2).reshape(rows)
 
-        tok = by_device(tokens)
         positions = by_device(lengths[None, :] + jnp.arange(steps, dtype=jnp.int32)[:, None])
         inv_freq = 10000.0 ** (-jnp.arange(half, dtype=F32) / half)
         ang = inv_freq[:, None] * positions[None, :].astype(F32)
@@ -457,11 +533,11 @@
         proj = (cos_t, sin_t, jnp.cos(ang_k), jnp.sin(ang_k), wkv_t, wq_t, w_gate, w_up)
         gains = [ln_scale[l][None] for l in range(layers)] + [final_scale[None]]
 
-        emb = lookup(tok - rank * vocab_local, embedding)
+        emb = lookup(n_dev, tokens, embedding)
         x, q_seq, hid, k_new, v_new = layer_step(n_dev, 0, (emb,), gains[0], proj, rows)
         outs = None
         for l in range(layers):
-            o, *outs = attention(l, steps, local_len, q_seq, k_new, v_new, kc, vc, outs)
+            o, *outs = attention(l, steps, lengths, q_seq, k_new, v_new, kc, vc, outs)
             ins = (o, hid, x, wo_r, w_down)
             if l + 1 < layers:
                 x, q_seq, hid, k_new, v_new = layer_step(n_dev, l + 1, ins, gains[l + 1], proj, rows)

time: 179 us -> 148 us (0.83)
  local copies, waits for them, and re-layouts: 26.1 us -> 3.68 us
  Pallas kernels: 150 us -> 141 us
    unnamed x34 -> x2, local copies, waits for them, and re-layouts: 24.2 us -> 0.01 us
    pallas_call x3, Pallas kernels: 117 us -> 108 us  [layer_step(): pl.pallas_call(functools.partial(layer_kernel, n_dev, layer, first, last)...]
    pallas_call x1, Pallas kernels: 7.01 us -> 11.1 us  [output_head(): pl.pallas_call(functools.partial(logits_kernel, n_dev, seqs, dim ** (-0.5...]
    pallas_call x1, Pallas kernels: 10.4 us -> 7.04 us  [lookup(): pl.pallas_call(functools.partial(lookup_kernel, n_dev), out_shape=jax.Sha...]
where the time goes in v4:
time: 148 us; the launch traced here: 147 us
  Pallas kernels  141 us (95%)
  local copies, waits for them, and re-layouts  3.68 us (2%)
  other arithmetic  1.68 us (1%)
    pallas_call x3, Pallas kernels, layer_step(): pl.pallas_call(functools.partial(layer_kernel, n_dev, layer, first, last)...  108 us
    pallas_call x2, Pallas kernels, attention(): pl.pallas_call(functools.partial(attn_kernel, layer, outs is not None, st...  14.9 us
    pallas_call x1, Pallas kernels, output_head(): pl.pallas_call(functools.partial(logits_kernel, n_dev, seqs, dim ** (-0.5...  11.1 us
    pallas_call x1, Pallas kernels, lookup(): pl.pallas_call(functools.partial(lookup_kernel, n_dev), out_shape=jax.Sha...  7.04 us

profile of v4, /device:TPU:0, one launch (start us, length us, event | category | flops | bytes accessed | tf_op | source)
XLA Modules:
  0.0 147.3 jit_solution(11763188640458285485)
XLA Ops:
  0.6 0.7 dynamic_slice.3
  1.4 0.1 convert_element_type.25
  1.5 0.8 multiply_sine_fusion.1
  2.2 0.7 add.43
  3.0 0.1 convert_element_type.23
  3.1 0.9 multiply_sine_fusion
  4.0 1.4 fusion
  5.4 7.0 %lookup.1.refs_0_ = bf16[256,2560]{1,0:T(8,128)(2,1)} custom-call(s32[2,128]{1,0:T(2,128)} %tok_ref.1, bf16[3200,2560]{1,0:T(8,128)(2,1)} %e_ref.1), custom_call_target="tpu_custom_call" | custom-call | flops 1000000000 | bytes 2097152 | tf_op jit(solution)/shard_map/lookup/pallas_call | solution.py:341
  12.4 34.4 %layer0.1 = (bf16[16,2560]{1,0:T(8,128)(2,1)}, bf16[256,160]{1,0:T(8,128)(2,1)}, bf16[256,640]{1,0:T(8,128)(2,1)}, f32[80,16]{1,0:T(8,128)}, f32[80,16]{1,0:T(8,128)}) custom-call(bf16[256,2560]{1,0:T(8,128)(2,1)} %lookup.1.refs_0_, f32[1,2560]{1,0:T(1,128)} %get-tuple-element.36.refs_1_, f32[40,256]{1,0:T(8,128)} %get-tuple-element.38.refs_2_.refs_6_, ...), custom_call_target="tpu_custom_call" | custom-call | flops 20000000000 | bytes 16777216 | tf_op jit(solution)/shard_map/layer0/pallas_call | solution.py:492
  46.9 7.4 %attend0.1 = (bf16[256,160]{1,0:T(8,128)(2,1)}, bf16[2,8,80,2048]{3,2,1,0:T(8,128)(2,1)}, bf16[2,8,80,2048]{3,2,1,0:T(8,128)(2,1)}) custom-call(s32[128]{0:T(128)} %len_ref.3, bf16[256,160]{1,0:T(8,128)(2,1)} %get-tuple-element.19.q_ref, f32[80,16]{1,0:T(8,128)} %get-tuple-element.20.kn_ref, f32[80,16]{1,0:T(8,128)} %get-tuple-element.21.vn_ref, ...), custom_call_target="tpu_custom_call" | custom-call | flops 2000000000 | bytes 22020096 | tf_op jit(solution)/shard_map/attend0/pallas_call | solution.py:118
  54.3 39.4 %layer1.1 = (bf16[16,2560]{1,0:T(8,128)(2,1)}, bf16[256,160]{1,0:T(8,128)(2,1)}, bf16[256,640]{1,0:T(8,128)(2,1)}, f32[80,16]{1,0:T(8,128)}, f32[80,16]{1,0:T(8,128)}) custom-call(bf16[256,160]{1,0:T(8,128)(2,1)} %get-tuple-element.22.refs_0_, bf16[256,640]{1,0:T(8,128)(2,1)} %get-tuple-element.23.refs_1_, bf16[16,2560]{1,0:T(8,128)(2,1)} %get-tuple-element.24.refs_2_, ...), custom_call_target="tpu_custom_call" | custom-call | flops 20000000000 | bytes 16777216 | tf_op jit(solution)/shard_map/layer1/pallas_call | solution.py:492
  93.7 0.0 copy-start
  93.7 7.4 %attend1.1 = (bf16[256,160]{1,0:T(8,128)(2,1)}, bf16[2,8,80,2048]{3,2,1,0:T(8,128)(2,1)}, bf16[2,8,80,2048]{3,2,1,0:T(8,128)(2,1)}) custom-call(s32[128]{0:T(128)} %len_ref.3, bf16[256,160]{1,0:T(8,128)(2,1)} %get-tuple-element.25.q_ref, f32[80,16]{1,0:T(8,128)} %get-tuple-element.26.kn_ref, ...), custom_call_target="tpu_custom_call", output_to_operand_aliasing={{1}: (6, {}), {2}: (7, {})} | custom-call | flops 2000000000 | bytes 22020096 | tf_op jit(solution)/shard_map/attend1/pallas_call | solution.py:118
  101.2 0.0 copy-done
  101.2 0.6 broadcast_in_dim.2.refs_3_
  101.8 34.5 %layer2.1.h_ref = bf16[256,2560]{1,0:T(8,128)(2,1)} custom-call(bf16[256,160]{1,0:T(8,128)(2,1)} %get-tuple-element.30.refs_0_, bf16[256,640]{1,0:T(8,128)(2,1)} %get-tuple-element.31.refs_1_, bf16[16,2560]{1,0:T(8,128)(2,1)} %get-tuple-element.32.refs_2_, f32[1,2560]{1,0:T(1,128)} %broadcast_in_dim.2.refs_3_, bf16[2,160,2560]{2,1,0:T(8,128)(2,1)} %bitcast.20, ...), custom_call_target="tpu_custom_call" | custom-call | flops 20000000000 | bytes 16777216 | tf_op jit(solution)/shard_map/layer2/pallas_call | solution.py:492
  136.3 11.1 %head.1 = f32[2,128,3200]{2,1,0:T(8,128)} custom-call(bf16[256,2560]{1,0:T(8,128)(2,1)} %layer2.1.h_ref, bf16[3200,2560]{1,0:T(8,128)(2,1)} %e_ref.1), custom_call_target="tpu_custom_call" | custom-call | flops 4000000000 | bytes 20971520 | tf_op jit(solution)/shard_map/head/pallas_call | solution.py:366
  (3 shorter events, 0.0 us)
Async XLA Ops:
  93.7 7.5 %copy-start = (f32[2560]{0:T(1024)S(1)}, f32[2560]{0:T(1024)}, u32[]{:S(2)}) copy-start(f32[2560]{0:T(1024)} %param.23) | copy-start | bytes 30724
